TPU v7x, 512 devices: a whole 4x4x16 slice. The times are simulated.
512 devices in a mesh: dp: 64 (over z, x), head: 8 (over y, core).
Axes of the slice: x: 4, y: 4, z: 16, core: 2. Of those that a mesh axis runs over, the one named last changes fastest.
Arguments:
- queries: bfloat16 [16384, 8192], P('dp', 'head'), may hold values from -6 to 6
- keys: bfloat16 [16384, 1024], P('dp', 'head'), may hold values from -6 to 6
- values: bfloat16 [16384, 1024], P('dp', 'head'), may hold values from -6 to 6
- output_grad: bfloat16 [16384, 4096], P('dp', 'head'), may hold values from -6 to 6
- out_weight: bfloat16 [8192, 4096], P(('head', 'dp')), may hold values from -0.0625 to 0.0625
- lengths: int32 [64], replicated, may hold values from 1 to 512, 16384 in all
Outputs:
- layer_out: bfloat16 [16384, 4096], P('dp', 'head')
- query_grad: bfloat16 [16384, 8192], P('dp', 'head')
- key_grad: bfloat16 [16384, 1024], P('dp', 'head')
- value_grad: bfloat16 [16384, 1024], P('dp', 'head')
Inputs may be any that keep to these rules, and one draw needn't show every extreme that they name: Each of the 64 lengths is at least 1 and at most 512, they sum to 16384, and one equals 512.
All inputs are finite; a program needn't handle non-finite values.
Results may differ from a plain program's by a relative error of at most 0.028.
Values may be sent and summed in bfloat16 or wider, within the bound.
No kernel may reach another device: no remote copies, remote signals or barrier semaphores. Data moves between devices by JAX's collectives and lax.ppermute only.
A program may use at most 128 MiB of HBM per device.

v0:
```python
import functools
import math

import jax
import jax.numpy as jnp
from jax import lax
from jax.experimental import pallas as pl
from jax.experimental.pallas import tpu as pltpu
from jax.sharding import Mesh
from jax.sharding import PartitionSpec as P

HD = 128
LOG2E = 1.4426950408889634
NT = (((1,), (1,)), ((), ()))
HEAD = ("y", "core")
DP = ("z_far", "z_pair", "x")
BF = jnp.bfloat16
F32 = jnp.float32
HEADS = 8


def dot_nt(a, b):
    return lax.dot_general(a, b, NT, preferred_element_type=F32)


def dot_nn(a, b):
    return jnp.dot(a, b, preferred_element_type=F32)


def call(body, flops, **spec):
    return pl.pallas_call(
        body,
        compiler_params=pltpu.CompilerParams(dimension_semantics=("arbitrary",) * len(spec["grid"])),
        cost_estimate=pl.CostEstimate(flops=flops, transcendentals=0, bytes_accessed=8 << 20),
        **spec,
    )


def forward_body(scaling, group, lengths, place, q, k2, k1, k0, v2, v1, v0, att, shares, bias, vt):
    rows = q.shape[0]
    blocks = 3

    @pl.when(pl.program_id(0) == 0)
    def _():
        first = place[0] * rows
        at = first + lax.broadcasted_iota(jnp.int32, (1, rows), 1)

        def doc(d, carry):
            end, start = carry
            end = end + lengths[d]
            return end, jnp.where(end <= at, end, start)

        _, start = lax.fori_loop(0, lengths.shape[0], doc, (jnp.int32(0), jnp.zeros((1, rows), jnp.int32)))
        keyed = first - (blocks - 1) * rows + lax.broadcasted_iota(jnp.int32, (blocks * rows, rows), 0)
        bias[...] = jnp.where((keyed >= start) & (keyed <= at), 0.0, -1e30)
        for j, v in enumerate((v2, v1, v0)):
            vt[:, j * rows : (j + 1) * rows] = v[...].T

    for h in range(group):
        cols = slice(h * HD, (h + 1) * HD)
        qh = q[:, cols]
        s = [
            dot_nt(k[...], qh) * (scaling * LOG2E) + bias[j * rows : (j + 1) * rows, :]
            for j, k in enumerate((k2, k1, k0))
        ]
        top = functools.reduce(jnp.maximum, [jnp.max(x, axis=0, keepdims=True) for x in s])
        e = [jnp.exp2(x - top) for x in s]
        inv = 1.0 / sum(jnp.sum(x, axis=0, keepdims=True) for x in e)
        out = jnp.zeros((HD, rows), F32)
        for j, x in enumerate(e):
            p = (x * inv).astype(BF)
            shares[h, j * rows : (j + 1) * rows, :] = p
            out = out + dot_nn(vt[:, j * rows : (j + 1) * rows], p)
        att[:, cols] = out.T.astype(BF)


def pair_specs(rows):
    key, value = pl.BlockSpec((rows, HD), lambda i: (0, 0)), pl.BlockSpec((rows, HD), lambda i: (1, 0))
    return [key] * 3 + [value] * 3


def forward(lengths, place, q, pairs, group=2):
    rows, width = q.shape
    heads = width // HD
    smem = pl.BlockSpec(memory_space=pltpu.SMEM)
    return call(
        functools.partial(forward_body, 1.0 / math.sqrt(HD), group),
        8 << 30,
        grid=(heads // group,),
        in_specs=[smem, smem, pl.BlockSpec((rows, group * HD), lambda i: (0, i))] + pair_specs(rows),
        out_specs=[
            pl.BlockSpec((rows, group * HD), lambda i: (0, i)),
            pl.BlockSpec((group, 3 * rows, rows), lambda i: (i, 0, 0)),
        ],
        out_shape=[
            jax.ShapeDtypeStruct((rows, width), BF),
            jax.ShapeDtypeStruct((heads, 3 * rows, rows), BF),
        ],
        scratch_shapes=[pltpu.VMEM((3 * rows, rows), F32), pltpu.VMEM((HD, 3 * rows), BF)],
    )(lengths, place, q, *pairs, *pairs)


def backward_body(scaling, group, q, k2, k1, k0, v2, v1, v0, d0, d1, d2, d3, att, shares, dq, far2, far1, home, kt, dka, dva):
    rows = q.shape[0]
    step = pl.program_id(0)

    @pl.when(step == 0)
    def _():
        for j, k in enumerate((k2, k1, k0)):
            kt[:, j * rows : (j + 1) * rows] = k[...].T
        dka[...] = jnp.zeros_like(dka)
        dva[...] = jnp.zeros_like(dva)

    spans = [slice(h * HD, (h + 1) * HD) for h in range(group)]
    das = [sum(d[:, cols].astype(F32) for d in (d0, d1, d2, d3)).astype(BF) for cols in spans]
    prods = [da.astype(F32) * att[:, cols].astype(F32) for da, cols in zip(das, spans)]
    dots = [jnp.sum(prod.T, axis=0, keepdims=True) for prod in prods]
    stacked_q = jnp.concatenate([q[:, cols] for cols in spans], axis=0)
    stacked_da = jnp.concatenate(das, axis=0)
    outs = [jnp.zeros((HD, rows), F32)] * group
    for j, v in enumerate((v2, v1, v0)):
        own = slice(j * rows, (j + 1) * rows)
        low = [shares[h, own, :] for h in range(group)]
        ds = [(p.astype(F32) * (dot_nt(v[...], da) - dot)).astype(BF) for p, da, dot in zip(low, das, dots)]
        outs = [out + dot_nn(kt[:, own], d) for out, d in zip(outs, ds)]
        dka[own, :] += dot_nn(jnp.concatenate(ds, axis=1), stacked_q)
        dva[own, :] += dot_nn(jnp.concatenate(low, axis=1), stacked_da)
    for cols, out in zip(spans, outs):
        dq[:, cols] = (out.T * scaling).astype(BF)

    @pl.when(step == pl.num_programs(0) - 1)
    def _():
        for j, to in enumerate((far2, far1, home)):
            own = slice(j * rows, (j + 1) * rows)
            to[:rows, :] = (dka[own, :] * scaling).astype(to.dtype)
            to[rows:, :] = dva[own, :].astype(to.dtype)


def backward(q, pairs, d_parts, att, shares, group=2):
    rows, width = q.shape
    heads = width // HD
    head = pl.BlockSpec((rows, group * HD), lambda i: (0, i))
    pair = pl.BlockSpec((2 * rows, HD), lambda i: (0, 0))
    return call(
        functools.partial(backward_body, 1.0 / math.sqrt(HD), group),
        8 << 30,
        grid=(heads // group,),
        in_specs=[head]
        + pair_specs(rows)
        + [head] * (len(d_parts) + 1)
        + [pl.BlockSpec((group, 3 * rows, rows), lambda i: (i, 0, 0))],
        out_specs=[head] + [pair] * 3,
        out_shape=[jax.ShapeDtypeStruct((rows, width), BF)]
        + [jax.ShapeDtypeStruct((2 * rows, HD), t) for t in (BF, BF, F32)],
        scratch_shapes=[
            pltpu.VMEM((HD, 3 * rows), BF),
            pltpu.VMEM((3 * rows, HD), F32),
            pltpu.VMEM((3 * rows, HD), F32),
        ],
    )(q, *pairs, *pairs, *d_parts, att, shares)


def back_body(index, og, w, *refs):
    *outs, lhs = refs
    rows = outs[0].shape[0]

    @pl.when(pl.program_id(0) == 0)
    def _():
        for k in range(len(outs)):
            block = lax.rem(index[0] + k, len(outs))
            at = pl.ds(pl.multiple_of(block * rows, rows), rows)
            for h in range(og.shape[0]):
                lhs[k * rows : (k + 1) * rows, h * HD : (h + 1) * HD] = og[h, at, :]

    done = dot_nt(lhs[...], w[...]).astype(BF)
    for k, out in enumerate(outs):
        out[...] = done[k * rows : (k + 1) * rows]


def project_back(index, og, w, parts, block=256):
    _, tokens, _ = og.shape
    inner, columns = w.shape
    rows = tokens // parts
    return pl.pallas_call(
        back_body,
        grid_spec=pltpu.PrefetchScalarGridSpec(
            num_scalar_prefetch=1,
            grid=(inner // block,),
            in_specs=[
                pl.BlockSpec(memory_space=pltpu.VMEM),
                pl.BlockSpec((block, columns), lambda i, s: (i, 0)),
            ],
            out_specs=[pl.BlockSpec((rows, block), lambda i, s: (0, i))] * parts,
            scratch_shapes=[pltpu.VMEM((tokens, columns), BF)],
        ),
        out_shape=[jax.ShapeDtypeStruct((rows, inner), BF)] * parts,
        compiler_params=pltpu.CompilerParams(dimension_semantics=("arbitrary",)),
        cost_estimate=pl.CostEstimate(flops=2 << 30, transcendentals=0, bytes_accessed=8 << 20),
        name="project_back",
    )(index, og, w)


def out_body(parts, index, side, *refs):
    blocks, w0, w1, add = refs[:parts], refs[parts], refs[parts + 1], refs[parts + 3 : -2]
    out, lhs = refs[-2:]
    rows = blocks[0].shape[0]

    @pl.when(pl.program_id(0) == 0)
    def _():
        for k, block in enumerate(blocks):
            owner = lax.rem(index[0] + parts - k, parts)
            lhs[pl.ds(pl.multiple_of(owner * rows, rows), rows), :] = block[...]

    done = dot_nn(lhs[...], jnp.concatenate([w0[...], w1[...]], axis=1))
    for n in range(2):
        value = done[:, n * HD : (n + 1) * HD]
        for more in add:
            value = value + more[2 * pl.program_id(0) + n].astype(F32)
        out[n] = value.astype(BF)


def project_out(index, side, blocks, w, after, *add):
    rows, inner = blocks[0].shape
    parts = len(blocks)
    whole = pl.BlockSpec(memory_space=pltpu.VMEM)
    part = pl.BlockSpec((2, parts * rows, HD), lambda i, x, s: (i, 0, 0))
    columns = [pl.BlockSpec((inner, HD), lambda i, x, s, n=n: (0, 4 * i + 2 * n + s[0])) for n in range(2)]
    return pl.pallas_call(
        functools.partial(out_body, parts),
        grid_spec=pltpu.PrefetchScalarGridSpec(
            num_scalar_prefetch=2,
            grid=(HEADS // 4,),
            in_specs=[whole] * parts + columns + [pl.BlockSpec(memory_space=pl.ANY)] + [whole] * len(add),
            out_specs=part,
            scratch_shapes=[pltpu.VMEM((parts * rows, inner), BF)],
        ),
        out_shape=jax.ShapeDtypeStruct((HEADS // 2, parts * rows, HD), BF),
        compiler_params=pltpu.CompilerParams(dimension_semantics=("arbitrary",)),
        cost_estimate=pl.CostEstimate(flops=1 << 30, transcendentals=0, bytes_accessed=4 << 20),
        name="project_out",
    )(index, side, *blocks, w, w, after, *add)


def swap(pieces, axis):
    return lax.all_to_all(pieces, axis, 0, 0, tiled=True)


def everywhere(x, axis):
    return swap(jnp.broadcast_to(x[None], (lax.axis_size(axis), *x.shape)), axis)


def shifted(block, distance):
    size = lax.axis_size(DP)
    return lax.ppermute(block, DP, [(i, i + distance) for i in range(size) if 0 <= i + distance < size])


def partner(block, axis):
    return lax.ppermute(block, axis, [(i, i ^ 1) for i in range(lax.axis_size(axis))])


def around(blocks, axis, step):
    size = lax.axis_size(axis)
    return [blocks[0]] + [
        lax.ppermute(blocks[k], axis, [(i, (i + k * step) % size) for i in range(size)]) for k in range(1, size)
    ]


def on_device(queries, keys, values, output_grad, out_weight, lengths):
    rows = queries.shape[0]
    few = out_weight.shape[0]
    parts = lax.axis_size("x")
    place = lax.axis_index(DP).astype(jnp.int32).reshape(1)
    index = lax.axis_index("x").astype(jnp.int32).reshape(1)
    core = lax.axis_index("core").astype(jnp.int32).reshape(1)
    own_w = out_weight.reshape(few, HEADS, parts, HD).transpose(2, 0, 1, 3).reshape(parts, few, HEADS * HD)
    own_w = jnp.concatenate([own_w] * 2, axis=0)
    own_w = swap(own_w, ("z_pair", "x")).reshape(-1, HEADS * HD)
    weight = lax.all_gather(own_w, "z_far", axis=0, tiled=True)
    pair = jnp.concatenate([keys, values], axis=0)
    pairs = [shifted(pair, 2), shifted(pair, 1), pair]
    own_g = output_grad.reshape(rows, parts, HD).transpose(1, 0, 2)
    grads = swap(own_g, "x").reshape(parts * rows, HD)
    grads = everywhere(grads, HEAD)
    attended, shares = forward(lengths, place, queries, pairs)
    attended_all = around([attended] * parts, "x", 1)

    d_here = project_back(index, grads, weight, parts)
    d_parts = around(d_here, "x", 1)
    outward = project_out(index, 1 - core, attended_all, weight, d_here[0])
    outward = partner(outward, "core")
    projected = project_out(index, core, attended_all, weight, d_here[0], outward)
    projected = swap(projected, "y")
    projected = projected.astype(F32).sum(axis=0).astype(BF)
    feature_parts = swap(projected.reshape(parts, rows, HD), "x")
    query_grad, far2, far1, home = backward(queries, pairs, d_parts, attended, shares)
    two, one = shifted(far2, -2), shifted(far1, -1)
    home, feature_parts = lax.optimization_barrier((home, feature_parts))
    layer_out = jnp.concatenate([feature_parts[j] for j in range(parts)], axis=1)
    total = (home + two.astype(F32) + one.astype(F32)).astype(BF)
    return layer_out, query_grad, total[:rows], total[rows:]


def solution(mesh):
    finer = Mesh(mesh.devices.reshape(8, 2, 4, 4, 2), ("z_far", "z_pair", "x", "y", "core"))
    token = P(DP, HEAD)

    return jax.shard_map(
        on_device,
        mesh=finer,
        in_specs=(token, token, token, token, P((*HEAD, *DP), None), P()),
        out_specs=(token,) * 4,
        check_vma=False,
    )
```

profile of v0, /device:TPU:328, one launch (start us, length us, event | category | flops | bytes accessed | tf_op | source)
XLA Modules:
  0.0 183.9 jit_solution(6499108377513376165)
XLA Ops:
  8.4 11.9 %all_to_all.25 = bf16[8,16,1024]{2,1,0:T(8,128)(2,1)} all-to-all(bf16[8,16,1024]{2,1,0:T(8,128)(2,1)S(1)} %pad_maximum_fusion), channel_id=1, replica_groups=mesh['z_far'=8,'z_pair'=2,'x'=4,'y'=4,'core'=2] {'z_pair','x'}, dimensions={0} | all-to-all | bytes 524288 | tf_op jit(solution)/shard_map/all_to_all | solution.py:245
  20.6 9.1 %all_to_all.26 = bf16[4,256,128]{2,1,0:T(8,128)(2,1)S(1)} all-to-all(bf16[4,256,128]{2,1,0:T(8,128)(2,1)S(1)} %copy.14), channel_id=1, replica_groups=mesh['z_far'=8,'z_pair'=2,'x'=4,'y'=4,'core'=2] {'x'}, dimensions={0} | all-to-all | bytes 524288 | tf_op jit(solution)/shard_map/all_to_all | solution.py:245
  31.3 5.0 %all-to-all-start.1 = ((bf16[8,1024,128]{2,1,0:T(8,128)(2,1)}), bf16[8,1024,128]{2,1,0:T(8,128)(2,1)}, u32[]{:S(2)}, u32[]{:S(2)}) async-start(bf16[8,1024,128]{2,1,0:T(8,128)(2,1)} %broadcast_in_dim.8), calls=%async_computation.1 | async-start | bytes 4194304 | tf_op jit(solution)/shard_map/all_to_all | solution.py:245
  36.4 2.7 %collective-permute-start = (bf16[512,128]{1,0:T(8,128)(2,1)S(1)}, bf16[512,128]{1,0:T(8,128)(2,1)S(1)}, u32[]{:S(2)}, u32[]{:S(2)}) collective-permute-start(bf16[512,128]{1,0:T(8,128)(2,1)S(1)} %constant_dynamic-update-slice_fusion.k0.v0), channel_id=1, source_target_pairs={{0,16},{8,24},{16,32},{24,40},{32,48},{40,56},{48,64},{56,72},{64,... | collective-permute-start | bytes 393224 | tf_op jit(solution)/shard_map/ppermute | solution.py:254
  39.2 3.1 %collective-permute-start.1 = (bf16[512,128]{1,0:T(8,128)(2,1)S(1)}, bf16[512,128]{1,0:T(8,128)(2,1)S(1)}, u32[]{:S(2)}, u32[]{:S(2)}) collective-permute-start(bf16[512,128]{1,0:T(8,128)(2,1)S(1)} %constant_dynamic-update-slice_fusion.k0.v0), channel_id=1, source_target_pairs={{0,8},{8,16},{16,24},{24,32},{32,40},{40,48},{48,56},{56,64},{64,7... | collective-permute-start | bytes 393224 | tf_op jit(solution)/shard_map/ppermute | solution.py:254
  42.3 9.5 %collective-permute-done.k2.v2 = bf16[512,128]{1,0:T(8,128)(2,1)S(1)} collective-permute-done((bf16[512,128]{1,0:T(8,128)(2,1)S(1)}, bf16[512,128]{1,0:T(8,128)(2,1)S(1)}, u32[]{:S(2)}, u32[]{:S(2)}) %collective-permute-start) | collective-permute-done | bytes 131104 | tf_op jit(solution)/shard_map/ppermute | solution.py:254
  51.8 8.1 %collective-permute-done.1.k1.v1 = bf16[512,128]{1,0:T(8,128)(2,1)S(1)} collective-permute-done((bf16[512,128]{1,0:T(8,128)(2,1)S(1)}, bf16[512,128]{1,0:T(8,128)(2,1)S(1)}, u32[]{:S(2)}, u32[]{:S(2)}) %collective-permute-start.1) | collective-permute-done | bytes 131104 | tf_op jit(solution)/shard_map/ppermute | solution.py:254
  60.6 7.8 %shard_map.93 = (bf16[256,1024]{1,0:T(8,128)(2,1)}, bf16[8,768,256]{2,1,0:T(8,128)(2,1)}) custom-call(s32[64]{0:T(128)} %lengths.1, s32[1]{0:T(128)} %bitcast.6.place, bf16[256,1024]{1,0:T(8,128)(2,1)} %q.3, bf16[512,128]{1,0:T(8,128)(2,1)} %copy-done.12, bf16[512,128]{1,0:T(8,128)(2,1)} %copy-done.13, bf16[512,128]{1,0:T(8,128)(2,1)} %copy-done.7, ...), custom_call_target="tpu_custom_call" | custom-call | flops 8589934592 | bytes 8388608 | tf_op jit(solution)/shard_map/pallas_call | solution.py:86
  70.3 3.0 %collective-permute-start.6 = (bf16[256,1024]{1,0:T(8,128)(2,1)}, bf16[256,1024]{1,0:T(8,128)(2,1)S(1)}, u32[]{:S(2)}, u32[]{:S(2)}) collective-permute-start(bf16[256,1024]{1,0:T(8,128)(2,1)} %get-tuple-element.20.att.refs_0_), channel_id=1, source_target_pairs={{0,16},{8,24},{16,0},{24,8},{1,17},{9,25},{17,1},{25,9},{2,18},{10... | collective-permute-start | bytes 1572872 | tf_op jit(solution)/shard_map/ppermute | solution.py:264
  73.4 4.0 %collective-permute-start.7 = (bf16[256,1024]{1,0:T(8,128)(2,1)}, bf16[256,1024]{1,0:T(8,128)(2,1)S(1)}, u32[]{:S(2)}, u32[]{:S(2)}) collective-permute-start(bf16[256,1024]{1,0:T(8,128)(2,1)} %get-tuple-element.20.att.refs_0_), channel_id=1, source_target_pairs={{0,24},{8,0},{16,8},{24,16},{1,25},{9,1},{17,9},{25,17},{2,26},{10... | collective-permute-start | bytes 1572872 | tf_op jit(solution)/shard_map/ppermute | solution.py:264
  78.3 6.5 %project_back.1 = (bf16[256,1024]{1,0:T(8,128)(2,1)}, bf16[256,1024]{1,0:T(8,128)(2,1)}, bf16[256,1024]{1,0:T(8,128)(2,1)}, bf16[256,1024]{1,0:T(8,128)(2,1)}) custom-call(s32[1]{0:T(128)} %bitcast.index, bf16[8,1024,128]{2,1,0:T(8,128)(2,1)} %all-to-all-done.1.og, bf16[1024,1024]{1,0:T(8,128)(2,1)} %all-gather.2.cloned.1.call-done.w.refs_4_.refs_5_), custom_call_target="tpu_custom_call" | custom-call | flops 2147483648 | bytes 8388608 | tf_op jit(solution)/shard_map/project_back/pallas_call | solution.py:184
  84.7 11.4 %collective-permute-done.5.refs_1_ = bf16[256,1024]{1,0:T(8,128)(2,1)S(1)} collective-permute-done((bf16[256,1024]{1,0:T(8,128)(2,1)}, bf16[256,1024]{1,0:T(8,128)(2,1)S(1)}, u32[]{:S(2)}, u32[]{:S(2)}) %collective-permute-start.5) | collective-permute-done | bytes 524320 | tf_op jit(solution)/shard_map/ppermute | solution.py:264
  96.1 2.5 %collective-permute-done.7.refs_3_ = bf16[256,1024]{1,0:T(8,128)(2,1)S(1)} collective-permute-done((bf16[256,1024]{1,0:T(8,128)(2,1)}, bf16[256,1024]{1,0:T(8,128)(2,1)S(1)}, u32[]{:S(2)}, u32[]{:S(2)}) %collective-permute-start.7) | collective-permute-done | bytes 524320 | tf_op jit(solution)/shard_map/ppermute | solution.py:264
  99.5 4.1 %project_out.2 = bf16[4,1024,128]{2,1,0:T(8,128)(2,1)} custom-call(s32[1]{0:T(128)} %bitcast.index, s32[1]{0:T(128)S(6)} %sub.3.side, bf16[256,1024]{1,0:T(8,128)(2,1)} %get-tuple-element.20.att.refs_0_, bf16[256,1024]{1,0:T(8,128)(2,1)} %copy-done, bf16[256,1024]{1,0:T(8,128)(2,1)} %copy-done.1, bf16[256,1024]{1,0:T(8,128)(2,1)} %copy-done.2, ...), custom_call_target="tpu_custom_call" | custom-call | flops 1073741824 | bytes 4194304 | tf_op jit(solution)/shard_map/project_out/pallas_call | solution.py:228
  105.5 2.8 %collective-permute-done.8.refs_7_ = bf16[4,1024,128]{2,1,0:T(8,128)(2,1)S(1)} collective-permute-done((bf16[4,1024,128]{2,1,0:T(8,128)(2,1)}, bf16[4,1024,128]{2,1,0:T(8,128)(2,1)S(1)}, u32[]{:S(2)}, u32[]{:S(2)}) %collective-permute-start.8) | collective-permute-done | bytes 1048608 | tf_op jit(solution)/shard_map/ppermute | solution.py:258
  109.3 4.5 %project_out.3 = bf16[4,1024,128]{2,1,0:T(8,128)(2,1)} custom-call(s32[1]{0:T(128)} %bitcast.index, s32[1]{0:T(128)} %bitcast.7.side, bf16[256,1024]{1,0:T(8,128)(2,1)} %get-tuple-element.20.att.refs_0_, bf16[256,1024]{1,0:T(8,128)(2,1)} %copy-done, bf16[256,1024]{1,0:T(8,128)(2,1)} %copy-done.1, bf16[256,1024]{1,0:T(8,128)(2,1)} %copy-done.2, ...), custom_call_target="tpu_custom_call" | custom-call | flops 1073741824 | bytes 4194304 | tf_op jit(solution)/shard_map/project_out/pallas_call | solution.py:228
  113.8 4.9 %all-to-all-start.3 = ((bf16[4,1024,128]{2,1,0:T(8,128)(2,1)}), bf16[4,1024,128]{2,1,0:T(8,128)(2,1)S(1)}, u32[]{:S(2)}, u32[]{:S(2)}) async-start(bf16[4,1024,128]{2,1,0:T(8,128)(2,1)} %project_out.3), calls=%async_computation.3 | async-start | bytes 2097152 | tf_op jit(solution)/shard_map/all_to_all | solution.py:245
  120.9 5.8 %collective-permute-start.3 = (bf16[256,1024]{1,0:T(8,128)(2,1)S(1)}, bf16[256,1024]{1,0:T(8,128)(2,1)}, u32[]{:S(2)}, u32[]{:S(2)}) collective-permute-start(bf16[256,1024]{1,0:T(8,128)(2,1)S(1)} %copy-done.9), channel_id=1, source_target_pairs={{0,16},{8,24},{16,0},{24,8},{1,17},{9,25},{17,1},{25,9},{2,18},{10... | collective-permute-start | bytes 1572872 | tf_op jit(solution)/shard_map/ppermute | solution.py:264
  128.6 4.1 %all-to-all-done.3 = bf16[4,1024,128]{2,1,0:T(8,128)(2,1)S(1)} async-done(((bf16[4,1024,128]{2,1,0:T(8,128)(2,1)}), bf16[4,1024,128]{2,1,0:T(8,128)(2,1)S(1)}, u32[]{:S(2)}, u32[]{:S(2)}) %all-to-all-start.3) | async-done | bytes 1048608 | tf_op jit(solution)/shard_map/all_to_all | solution.py:245
  133.6 3.9 %all-to-all-start.4 = ((bf16[4,256,128]{2,1,0:T(8,128)(2,1)}), bf16[4,256,128]{2,1,0:T(8,128)(2,1)S(1)}, u32[]{:S(2)}, u32[]{:S(2)}) async-start(bf16[4,256,128]{2,1,0:T(8,128)(2,1)} %bitcast.8), calls=%async_computation.4 | async-start | bytes 524288 | tf_op jit(solution)/shard_map/all_to_all | solution.py:245
  137.5 11.4 %collective-permute-done.3.d2 = bf16[256,1024]{1,0:T(8,128)(2,1)} collective-permute-done((bf16[256,1024]{1,0:T(8,128)(2,1)S(1)}, bf16[256,1024]{1,0:T(8,128)(2,1)}, u32[]{:S(2)}, u32[]{:S(2)}) %collective-permute-start.3) | collective-permute-done | bytes 524320 | tf_op jit(solution)/shard_map/ppermute | solution.py:264
  150.5 8.1 %shard_map.94 = (bf16[256,1024]{1,0:T(8,128)(2,1)}, bf16[512,128]{1,0:T(8,128)(2,1)}, bf16[512,128]{1,0:T(8,128)(2,1)}, f32[512,128]{1,0:T(8,128)}) custom-call(bf16[256,1024]{1,0:T(8,128)(2,1)} %q.3, bf16[512,128]{1,0:T(8,128)(2,1)} %copy-done.12, bf16[512,128]{1,0:T(8,128)(2,1)} %copy-done.13, bf16[512,128]{1,0:T(8,128)(2,1)} %copy-done.7, ...), custom_call_target="tpu_custom_call" | custom-call | flops 8589934592 | bytes 8388608 | tf_op jit(solution)/shard_map/pallas_call | solution.py:144
  158.7 7.4 %collective-permute-start.10 = (bf16[512,128]{1,0:T(8,128)(2,1)}, bf16[512,128]{1,0:T(8,128)(2,1)S(1)}, u32[]{:S(2)}, u32[]{:S(2)}) collective-permute-start(bf16[512,128]{1,0:T(8,128)(2,1)} %get-tuple-element.27), channel_id=1, source_target_pairs={{8,0},{16,8},{24,16},{32,24},{40,32},{48,40},{56,48},{64,56},{72,6... | collective-permute-start | bytes 393224 | tf_op jit(solution)/shard_map/ppermute | solution.py:254
  169.9 4.7 %collective-permute-done.9 = bf16[512,128]{1,0:T(8,128)(2,1)S(1)} collective-permute-done((bf16[512,128]{1,0:T(8,128)(2,1)}, bf16[512,128]{1,0:T(8,128)(2,1)S(1)}, u32[]{:S(2)}, u32[]{:S(2)}) %collective-permute-start.9) | collective-permute-done | bytes 131104 | tf_op jit(solution)/shard_map/ppermute | solution.py:254
  (56 shorter events, 23.1 us)
Async XLA Ops:
  7.2 13.1 %copy-start.4 = (bf16[256,512]{1,0:T(8,128)(2,1)S(1)}, bf16[256,512]{1,0:T(8,128)(2,1)}, u32[]{:S(2)}) copy-start(bf16[256,512]{1,0:T(8,128)(2,1)} %param.9) | copy-start | bytes 786436
  7.2 71.1 %all-gather.2.cloned.1.call-start = ((), (), s32[]{:S(2)}) async-start(), calls=%async_computation.5 | async-start | bytes 2359296 | tf_op jit(solution)/shard_map/all_gather | solution.py:278
  31.3 5.1 %copy-start.5 = (bf16[256,128]{1,0:T(8,128)(2,1)S(1)}, bf16[256,128]{1,0:T(8,128)(2,1)}, u32[]{:S(2)}) copy-start(bf16[256,128]{1,0:T(8,128)(2,1)} %param.7) | copy-start | bytes 196612
  31.3 5.1 %copy-start.6 = (bf16[256,128]{1,0:T(8,128)(2,1)S(1)}, bf16[256,128]{1,0:T(8,128)(2,1)}, u32[]{:S(2)}) copy-start(bf16[256,128]{1,0:T(8,128)(2,1)} %param.8) | copy-start | bytes 196612
  31.3 46.0 %all-to-all-start.1 = ((bf16[8,1024,128]{2,1,0:T(8,128)(2,1)}), bf16[8,1024,128]{2,1,0:T(8,128)(2,1)}, u32[]{:S(2)}, u32[]{:S(2)}) async-start(bf16[8,1024,128]{2,1,0:T(8,128)(2,1)} %broadcast_in_dim.8), calls=%async_computation.1 | async-start | bytes 4194304 | tf_op jit(solution)/shard_map/all_to_all | solution.py:245
  36.4 23.5 %copy-start.7 = (bf16[512,128]{1,0:T(8,128)(2,1)}, bf16[512,128]{1,0:T(8,128)(2,1)S(1)}, u32[]{:S(2)}) copy-start(bf16[512,128]{1,0:T(8,128)(2,1)S(1)} %constant_dynamic-update-slice_fusion.k0.v0) | copy-start | bytes 393220
  36.4 15.4 %collective-permute-start = (bf16[512,128]{1,0:T(8,128)(2,1)S(1)}, bf16[512,128]{1,0:T(8,128)(2,1)S(1)}, u32[]{:S(2)}, u32[]{:S(2)}) collective-permute-start(bf16[512,128]{1,0:T(8,128)(2,1)S(1)} %constant_dynamic-update-slice_fusion.k0.v0), channel_id=1, source_target_pairs={{0,16},{8,24},{16,32},{24,40},{32,48},{40,56},{48,64},{56,72},{64,... | collective-permute-start | bytes 393224 | tf_op jit(solution)/shard_map/ppermute | solution.py:254
  39.2 20.8 %collective-permute-start.1 = (bf16[512,128]{1,0:T(8,128)(2,1)S(1)}, bf16[512,128]{1,0:T(8,128)(2,1)S(1)}, u32[]{:S(2)}, u32[]{:S(2)}) collective-permute-start(bf16[512,128]{1,0:T(8,128)(2,1)S(1)} %constant_dynamic-update-slice_fusion.k0.v0), channel_id=1, source_target_pairs={{0,8},{8,16},{16,24},{24,32},{32,40},{40,48},{48,56},{56,64},{64,7... | collective-permute-start | bytes 393224 | tf_op jit(solution)/shard_map/ppermute | solution.py:254
  51.8 8.1 %copy-start.12 = (bf16[512,128]{1,0:T(8,128)(2,1)}, bf16[512,128]{1,0:T(8,128)(2,1)S(1)}, u32[]{:S(2)}) copy-start(bf16[512,128]{1,0:T(8,128)(2,1)S(1)} %collective-permute-done.k2.v2) | copy-start | bytes 393220
  68.4 27.7 %collective-permute-start.5 = (bf16[256,1024]{1,0:T(8,128)(2,1)}, bf16[256,1024]{1,0:T(8,128)(2,1)S(1)}, u32[]{:S(2)}, u32[]{:S(2)}) collective-permute-start(bf16[256,1024]{1,0:T(8,128)(2,1)} %get-tuple-element.20.att.refs_0_), channel_id=1, source_target_pairs={{0,8},{8,16},{16,24},{24,0},{1,9},{9,17},{17,25},{25,1},{2,10},{10... | collective-permute-start | bytes 1572872 | tf_op jit(solution)/shard_map/ppermute | solution.py:264
  70.3 25.8 %collective-permute-start.6 = (bf16[256,1024]{1,0:T(8,128)(2,1)}, bf16[256,1024]{1,0:T(8,128)(2,1)S(1)}, u32[]{:S(2)}, u32[]{:S(2)}) collective-permute-start(bf16[256,1024]{1,0:T(8,128)(2,1)} %get-tuple-element.20.att.refs_0_), channel_id=1, source_target_pairs={{0,16},{8,24},{16,0},{24,8},{1,17},{9,25},{17,1},{25,9},{2,18},{10... | collective-permute-start | bytes 1572872 | tf_op jit(solution)/shard_map/ppermute | solution.py:264
  73.4 25.3 %collective-permute-start.7 = (bf16[256,1024]{1,0:T(8,128)(2,1)}, bf16[256,1024]{1,0:T(8,128)(2,1)S(1)}, u32[]{:S(2)}, u32[]{:S(2)}) collective-permute-start(bf16[256,1024]{1,0:T(8,128)(2,1)} %get-tuple-element.20.att.refs_0_), channel_id=1, source_target_pairs={{0,24},{8,0},{16,8},{24,16},{1,25},{9,1},{17,9},{25,17},{2,26},{10... | collective-permute-start | bytes 1572872 | tf_op jit(solution)/shard_map/ppermute | solution.py:264
  103.6 4.8 %collective-permute-start.8 = (bf16[4,1024,128]{2,1,0:T(8,128)(2,1)}, bf16[4,1024,128]{2,1,0:T(8,128)(2,1)S(1)}, u32[]{:S(2)}, u32[]{:S(2)}) collective-permute-start(bf16[4,1024,128]{2,1,0:T(8,128)(2,1)} %project_out.2), channel_id=1, source_target_pairs={{0,1},{1,0},{2,3},{3,2},{4,5},{5,4},{6,7},{7,6},{8,9},{9,8},{10,11... | collective-permute-start | bytes 3145736 | tf_op jit(solution)/shard_map/ppermute | solution.py:258
  113.8 5.0 %copy-start.10 = (bf16[256,1024]{1,0:T(8,128)(2,1)S(1)}, bf16[256,1024]{1,0:T(8,128)(2,1)}, u32[]{:S(2)}) copy-start(bf16[256,1024]{1,0:T(8,128)(2,1)} %get-tuple-element.17) | copy-start | bytes 1572868
  113.8 7.1 %copy-start.9 = (bf16[256,1024]{1,0:T(8,128)(2,1)S(1)}, bf16[256,1024]{1,0:T(8,128)(2,1)}, u32[]{:S(2)}) copy-start(bf16[256,1024]{1,0:T(8,128)(2,1)} %get-tuple-element.18) | copy-start | bytes 1572868
  113.8 12.9 %copy-start.8 = (bf16[256,1024]{1,0:T(8,128)(2,1)S(1)}, bf16[256,1024]{1,0:T(8,128)(2,1)}, u32[]{:S(2)}) copy-start(bf16[256,1024]{1,0:T(8,128)(2,1)} %get-tuple-element.19) | copy-start | bytes 1572868
  113.8 18.9 %all-to-all-start.3 = ((bf16[4,1024,128]{2,1,0:T(8,128)(2,1)}), bf16[4,1024,128]{2,1,0:T(8,128)(2,1)S(1)}, u32[]{:S(2)}, u32[]{:S(2)}) async-start(bf16[4,1024,128]{2,1,0:T(8,128)(2,1)} %project_out.3), calls=%async_computation.3 | async-start | bytes 2097152 | tf_op jit(solution)/shard_map/all_to_all | solution.py:245
  118.7 18.7 %collective-permute-start.2 = (bf16[256,1024]{1,0:T(8,128)(2,1)S(1)}, bf16[256,1024]{1,0:T(8,128)(2,1)S(1)}, u32[]{:S(2)}, u32[]{:S(2)}) collective-permute-start(bf16[256,1024]{1,0:T(8,128)(2,1)S(1)} %copy-done.10), channel_id=1, source_target_pairs={{0,8},{8,16},{16,24},{24,0},{1,9},{9,17},{17,25},{25,1},{2,10},{10... | collective-permute-start | bytes 1572872 | tf_op jit(solution)/shard_map/ppermute | solution.py:264
  120.9 28.0 %collective-permute-start.3 = (bf16[256,1024]{1,0:T(8,128)(2,1)S(1)}, bf16[256,1024]{1,0:T(8,128)(2,1)}, u32[]{:S(2)}, u32[]{:S(2)}) collective-permute-start(bf16[256,1024]{1,0:T(8,128)(2,1)S(1)} %copy-done.9), channel_id=1, source_target_pairs={{0,16},{8,24},{16,0},{24,8},{1,17},{9,25},{17,1},{25,9},{2,18},{10... | collective-permute-start | bytes 1572872 | tf_op jit(solution)/shard_map/ppermute | solution.py:264
  126.7 23.9 %collective-permute-start.4 = (bf16[256,1024]{1,0:T(8,128)(2,1)S(1)}, bf16[256,1024]{1,0:T(8,128)(2,1)}, u32[]{:S(2)}, u32[]{:S(2)}) collective-permute-start(bf16[256,1024]{1,0:T(8,128)(2,1)S(1)} %copy-done.8), channel_id=1, source_target_pairs={{0,24},{8,0},{16,8},{24,16},{1,25},{9,1},{17,9},{25,17},{2,26},{10... | collective-permute-start | bytes 1572872 | tf_op jit(solution)/shard_map/ppermute | solution.py:264
  133.6 34.4 %all-to-all-start.4 = ((bf16[4,256,128]{2,1,0:T(8,128)(2,1)}), bf16[4,256,128]{2,1,0:T(8,128)(2,1)S(1)}, u32[]{:S(2)}, u32[]{:S(2)}) async-start(bf16[4,256,128]{2,1,0:T(8,128)(2,1)} %bitcast.8), calls=%async_computation.4 | async-start | bytes 524288 | tf_op jit(solution)/shard_map/all_to_all | solution.py:245
  137.5 13.1 %copy-start.11 = (bf16[256,1024]{1,0:T(8,128)(2,1)}, bf16[256,1024]{1,0:T(8,128)(2,1)S(1)}, u32[]{:S(2)}) copy-start(bf16[256,1024]{1,0:T(8,128)(2,1)S(1)} %collective-permute-done.2.d1) | copy-start | bytes 1572868
  158.7 11.2 %collective-permute-start.10 = (bf16[512,128]{1,0:T(8,128)(2,1)}, bf16[512,128]{1,0:T(8,128)(2,1)S(1)}, u32[]{:S(2)}, u32[]{:S(2)}) collective-permute-start(bf16[512,128]{1,0:T(8,128)(2,1)} %get-tuple-element.27), channel_id=1, source_target_pairs={{8,0},{16,8},{24,16},{32,24},{40,32},{48,40},{56,48},{64,56},{72,6... | collective-permute-start | bytes 393224 | tf_op jit(solution)/shard_map/ppermute | solution.py:254
  166.0 8.6 %collective-permute-start.9 = (bf16[512,128]{1,0:T(8,128)(2,1)}, bf16[512,128]{1,0:T(8,128)(2,1)S(1)}, u32[]{:S(2)}, u32[]{:S(2)}) collective-permute-start(bf16[512,128]{1,0:T(8,128)(2,1)} %get-tuple-element.26), channel_id=1, source_target_pairs={{16,0},{24,8},{32,16},{40,24},{48,32},{56,40},{64,48},{72,56},{80,... | collective-permute-start | bytes 393224 | tf_op jit(solution)/shard_map/ppermute | solution.py:254
  (5 other events, 7.5 us)
Sparse Core Ops, SparseCore 0:
  20.4 57.8 all-gather.1
where the time goes:
time: 185 us; the launch traced here: 184 us
  waiting for transfers between devices  59.1 us (32%)
  starting transfers between devices  49.7 us (27%)
  Pallas kernels  31 us (17%)
  blocking collectives  20.9 us (11%)
  between operations  14.3 us (8%)
  local copies, waits for them, and re-layouts  6.2 us (3%)
  other arithmetic  2.65 us (1%)
    ppermute x6, waiting for transfers between devices, around(): lax.ppermute(blocks[k], axis, [(i, (i + k * step) % size) for i in range(...  27 us
    ppermute x4, waiting for transfers between devices, shifted(): lax.ppermute(block, DP, [(i, i + distance) for i in range(size) if 0 <= i...  24.3 us
    all_to_all x2, blocking collectives, swap(): return lax.all_to_all(pieces, axis, 0, 0, tiled=True)  20.9 us
    ppermute x6, starting transfers between devices, around(): lax.ppermute(blocks[k], axis, [(i, (i + k * step) % size) for i in range(...  18.8 us
    ppermute x4, starting transfers between devices, shifted(): lax.ppermute(block, DP, [(i, i + distance) for i in range(size) if 0 <= i...  15.1 us
    all_to_all x3, starting transfers between devices, swap(): return lax.all_to_all(pieces, axis, 0, 0, tiled=True)  13.9 us
    pallas_call x2, Pallas kernels, project_out(): pl.pallas_call(functools.partial(out_body, parts), grid_spec=pltpu.Prefet...  8.6 us
    pallas_call x1, Pallas kernels, backward(): call(functools.partial(backward_body, 1.0 / math.sqrt(HD), group), 8 << 3...  8.14 us
  transfers between devices with their start and end apart: 15, of which 11 were waited for; matrix products, arithmetic and copies ran while one was open for 2% of the time, Pallas kernels for 12%

commit v1 on v0

--- a/solution.py
+++ b/solution.py
@@ -100,7 +100,7 @@
     )(lengths, place, q, *pairs, *pairs)
 
 
-def backward_body(scaling, group, q, k2, k1, k0, v2, v1, v0, d0, d1, d2, d3, att, shares, dq, far2, far1, home, kt, dka, dva):
+def backward_body(scaling, group, q, k2, k1, k0, v2, v1, v0, d_parts, att, shares, dq, far2, far1, home, kt, dka, dva):
     rows = q.shape[0]
     step = pl.program_id(0)
 
@@ -112,7 +112,7 @@
         dva[...] = jnp.zeros_like(dva)
 
     spans = [slice(h * HD, (h + 1) * HD) for h in range(group)]
-    das = [sum(d[:, cols].astype(F32) for d in (d0, d1, d2, d3)).astype(BF) for cols in spans]
+    das = [sum(d_parts[i, :, cols].astype(F32) for i in range(d_parts.shape[0])).astype(BF) for cols in spans]
     prods = [da.astype(F32) * att[:, cols].astype(F32) for da, cols in zip(das, spans)]
     dots = [jnp.sum(prod.T, axis=0, keepdims=True) for prod in prods]
     stacked_q = jnp.concatenate([q[:, cols] for cols in spans], axis=0)
@@ -147,7 +147,7 @@
         grid=(heads // group,),
         in_specs=[head]
         + pair_specs(rows)
-        + [head] * (len(d_parts) + 1)
+        + [pl.BlockSpec((d_parts.shape[0], rows, group * HD), lambda i: (0, 0, i)), head]
         + [pl.BlockSpec((group, 3 * rows, rows), lambda i: (i, 0, 0))],
         out_specs=[head] + [pair] * 3,
         out_shape=[jax.ShapeDtypeStruct((rows, width), BF)]
@@ -157,47 +157,34 @@
             pltpu.VMEM((3 * rows, HD), F32),
             pltpu.VMEM((3 * rows, HD), F32),
         ],
-    )(q, *pairs, *pairs, *d_parts, att, shares)
-
-
-def back_body(index, og, w, *refs):
-    *outs, lhs = refs
-    rows = outs[0].shape[0]
-
+    )(q, *pairs, *pairs, d_parts, att, shares)
+
+
+def back_body(og, w, out, lhs):
     @pl.when(pl.program_id(0) == 0)
     def _():
-        for k in range(len(outs)):
-            block = lax.rem(index[0] + k, len(outs))
-            at = pl.ds(pl.multiple_of(block * rows, rows), rows)
-            for h in range(og.shape[0]):
-                lhs[k * rows : (k + 1) * rows, h * HD : (h + 1) * HD] = og[h, at, :]
-
+        for h in range(og.shape[0]):
+            lhs[:, h * HD : (h + 1) * HD] = og[h]
+
+    rows = out.shape[1]
     done = dot_nt(lhs[...], w[...]).astype(BF)
-    for k, out in enumerate(outs):
-        out[...] = done[k * rows : (k + 1) * rows]
-
-
-def project_back(index, og, w, parts, block=256):
+    for b in range(out.shape[0]):
+        out[b] = done[b * rows : (b + 1) * rows]
+
+
+def project_back(og, w, parts, block=256):
     _, tokens, _ = og.shape
     inner, columns = w.shape
     rows = tokens // parts
-    return pl.pallas_call(
+    return call(
         back_body,
-        grid_spec=pltpu.PrefetchScalarGridSpec(
-            num_scalar_prefetch=1,
-            grid=(inner // block,),
-            in_specs=[
-                pl.BlockSpec(memory_space=pltpu.VMEM),
-                pl.BlockSpec((block, columns), lambda i, s: (i, 0)),
-            ],
-            out_specs=[pl.BlockSpec((rows, block), lambda i, s: (0, i))] * parts,
-            scratch_shapes=[pltpu.VMEM((tokens, columns), BF)],
-        ),
-        out_shape=[jax.ShapeDtypeStruct((rows, inner), BF)] * parts,
-        compiler_params=pltpu.CompilerParams(dimension_semantics=("arbitrary",)),
-        cost_estimate=pl.CostEstimate(flops=2 << 30, transcendentals=0, bytes_accessed=8 << 20),
-        name="project_back",
-    )(index, og, w)
+        2 << 30,
+        grid=(inner // block,),
+        in_specs=[pl.BlockSpec(memory_space=pltpu.VMEM), pl.BlockSpec((block, columns), lambda i: (i, 0))],
+        out_specs=pl.BlockSpec((parts, rows, block), lambda i: (0, 0, i)),
+        out_shape=jax.ShapeDtypeStruct((parts, rows, inner), BF),
+        scratch_shapes=[pltpu.VMEM((tokens, columns), BF)],
+    )(og, w)
 
 
 def out_body(parts, index, side, *refs):
@@ -284,11 +271,11 @@
     attended, shares = forward(lengths, place, queries, pairs)
     attended_all = around([attended] * parts, "x", 1)
 
-    d_here = project_back(index, grads, weight, parts)
-    d_parts = around(d_here, "x", 1)
-    outward = project_out(index, 1 - core, attended_all, weight, d_here[0])
+    d_here = project_back(grads, weight, parts)
+    d_parts = swap(d_here, "x")
+    outward = project_out(index, 1 - core, attended_all, weight, d_here)
     outward = partner(outward, "core")
-    projected = project_out(index, core, attended_all, weight, d_here[0], outward)
+    projected = project_out(index, core, attended_all, weight, d_here, outward)
     projected = swap(projected, "y")
     projected = projected.astype(F32).sum(axis=0).astype(BF)
     feature_parts = swap(projected.reshape(parts, rows, HD), "x")

time: 185 us -> 201 us (1.086)
  the two profiles are of different devices: /device:TPU:328 before, /device:TPU:384 now
where the time goes in v1:
time: 201 us; the launch traced here: 200 us
  waiting for transfers between devices  66.2 us (33%)
  blocking collectives  40.4 us (20%)
  starting transfers between devices  38.8 us (19%)
  Pallas kernels  31.2 us (16%)
  between operations  14.3 us (7%)
  local copies, waits for them, and re-layouts  6.41 us (3%)
  other arithmetic  2.65 us (1%)
    all_to_all x3, blocking collectives, swap(): return lax.all_to_all(pieces, axis, 0, 0, tiled=True)  40.4 us
    ppermute x4, waiting for transfers between devices, shifted(): lax.ppermute(block, DP, [(i, i + distance) for i in range(size) if 0 <= i...  25 us
    all_to_all x3, waiting for transfers between devices, swap(): return lax.all_to_all(pieces, axis, 0, 0, tiled=True)  24.3 us
    ppermute x4, starting transfers between devices, shifted(): lax.ppermute(block, DP, [(i, i + distance) for i in range(size) if 0 <= i...  15.9 us
    ppermute x3, waiting for transfers between devices, around(): lax.ppermute(blocks[k], axis, [(i, (i + k * step) % size) for i in range(...  13.6 us
    all_to_all x3, starting transfers between devices, swap(): return lax.all_to_all(pieces, axis, 0, 0, tiled=True)  11.9 us
    ppermute x3, starting transfers between devices, around(): lax.ppermute(blocks[k], axis, [(i, (i + k * step) % size) for i in range(...  8.96 us
    pallas_call x2, Pallas kernels, project_out(): pl.pallas_call(functools.partial(out_body, parts), grid_spec=pltpu.Prefet...  8.65 us
  transfers between devices with their start and end apart: 12, of which 9 were waited for; matrix products, arithmetic and copies ran while one was open for 1% of the time, Pallas kernels for 11%

profile of v1, /device:TPU:384, one launch (start us, length us, event | category | flops | bytes accessed | tf_op | source)
XLA Modules:
  0.0 199.9 jit_solution(4961732521850728978)
XLA Ops:
  8.4 11.9 %all_to_all.30 = bf16[8,16,1024]{2,1,0:T(8,128)(2,1)} all-to-all(bf16[8,16,1024]{2,1,0:T(8,128)(2,1)S(1)} %pad_maximum_fusion), channel_id=1, replica_groups=mesh['z_far'=8,'z_pair'=2,'x'=4,'y'=4,'core'=2] {'z_pair','x'}, dimensions={0} | all-to-all | bytes 524288 | tf_op jit(solution)/shard_map/all_to_all | solution.py:232
  20.6 9.1 %all_to_all.31 = bf16[4,256,128]{2,1,0:T(8,128)(2,1)S(1)} all-to-all(bf16[4,256,128]{2,1,0:T(8,128)(2,1)S(1)} %copy.14), channel_id=1, replica_groups=mesh['z_far'=8,'z_pair'=2,'x'=4,'y'=4,'core'=2] {'x'}, dimensions={0} | all-to-all | bytes 524288 | tf_op jit(solution)/shard_map/all_to_all | solution.py:232
  31.3 4.6 %all-to-all-start.1 = ((bf16[8,1024,128]{2,1,0:T(8,128)(2,1)}), bf16[8,1024,128]{2,1,0:T(8,128)(2,1)S(1)}, u32[]{:S(2)}, u32[]{:S(2)}) async-start(bf16[8,1024,128]{2,1,0:T(8,128)(2,1)} %broadcast_in_dim.8), calls=%async_computation.1 | async-start | bytes 4194304 | tf_op jit(solution)/shard_map/all_to_all | solution.py:232
  35.9 2.7 %collective-permute-start = (bf16[512,128]{1,0:T(8,128)(2,1)S(1)}, bf16[512,128]{1,0:T(8,128)(2,1)S(1)}, u32[]{:S(2)}, u32[]{:S(2)}) collective-permute-start(bf16[512,128]{1,0:T(8,128)(2,1)S(1)} %constant_dynamic-update-slice_fusion.k0.v0), channel_id=1, source_target_pairs={{0,16},{8,24},{16,32},{24,40},{32,48},{40,56},{48,64},{56,72},{64,... | collective-permute-start | bytes 393224 | tf_op jit(solution)/shard_map/ppermute | solution.py:241
  38.7 3.1 %collective-permute-start.1 = (bf16[512,128]{1,0:T(8,128)(2,1)S(1)}, bf16[512,128]{1,0:T(8,128)(2,1)S(1)}, u32[]{:S(2)}, u32[]{:S(2)}) collective-permute-start(bf16[512,128]{1,0:T(8,128)(2,1)S(1)} %constant_dynamic-update-slice_fusion.k0.v0), channel_id=1, source_target_pairs={{0,8},{8,16},{16,24},{24,32},{32,40},{40,48},{48,56},{56,64},{64,7... | collective-permute-start | bytes 393224 | tf_op jit(solution)/shard_map/ppermute | solution.py:241
  41.8 11.1 %collective-permute-done.k2.v2 = bf16[512,128]{1,0:T(8,128)(2,1)S(1)} collective-permute-done((bf16[512,128]{1,0:T(8,128)(2,1)S(1)}, bf16[512,128]{1,0:T(8,128)(2,1)S(1)}, u32[]{:S(2)}, u32[]{:S(2)}) %collective-permute-start) | collective-permute-done | bytes 131104 | tf_op jit(solution)/shard_map/ppermute | solution.py:241
  52.9 8.1 %collective-permute-done.1.k1.v1 = bf16[512,128]{1,0:T(8,128)(2,1)S(1)} collective-permute-done((bf16[512,128]{1,0:T(8,128)(2,1)S(1)}, bf16[512,128]{1,0:T(8,128)(2,1)S(1)}, u32[]{:S(2)}, u32[]{:S(2)}) %collective-permute-start.1) | collective-permute-done | bytes 131104 | tf_op jit(solution)/shard_map/ppermute | solution.py:241
  61.7 7.8 %shard_map.94 = (bf16[256,1024]{1,0:T(8,128)(2,1)}, bf16[8,768,256]{2,1,0:T(8,128)(2,1)}) custom-call(s32[64]{0:T(128)} %lengths.1, s32[1]{0:T(128)} %bitcast.5.place, bf16[256,1024]{1,0:T(8,128)(2,1)} %q.3, bf16[512,128]{1,0:T(8,128)(2,1)} %copy-done.9, bf16[512,128]{1,0:T(8,128)(2,1)} %copy-done.10, bf16[512,128]{1,0:T(8,128)(2,1)} %copy-done.8, ...), custom_call_target="tpu_custom_call" | custom-call | flops 8589934592 | bytes 8388608 | tf_op jit(solution)/shard_map/pallas_call | solution.py:86
  71.4 1.9 collective-permute-start.3
  73.3 5.1 %collective-permute-start.4 = (bf16[256,1024]{1,0:T(8,128)(2,1)}, bf16[256,1024]{1,0:T(8,128)(2,1)}, u32[]{:S(2)}, u32[]{:S(2)}) collective-permute-start(bf16[256,1024]{1,0:T(8,128)(2,1)} %get-tuple-element.12.att.refs_0_), channel_id=1, source_target_pairs={{0,24},{8,0},{16,8},{24,16},{1,25},{9,1},{17,9},{25,17},{2,26},{10... | collective-permute-start | bytes 1572872 | tf_op jit(solution)/shard_map/ppermute | solution.py:251
  79.9 6.8 %shard_map.93.refs_6_ = bf16[4,256,1024]{2,1,0:T(8,128)(2,1)} custom-call(bf16[8,1024,128]{2,1,0:T(8,128)(2,1)} %copy-done, bf16[1024,1024]{1,0:T(8,128)(2,1)} %all-gather.2.cloned.1.call-done.w.refs_4_.refs_5_), custom_call_target="tpu_custom_call" | custom-call | flops 2147483648 | bytes 8388608 | tf_op jit(solution)/shard_map/pallas_call | solution.py:179
  86.6 11.0 %collective-permute-done.2.refs_1_ = bf16[256,1024]{1,0:T(8,128)(2,1)S(1)} collective-permute-done((bf16[256,1024]{1,0:T(8,128)(2,1)}, bf16[256,1024]{1,0:T(8,128)(2,1)S(1)}, u32[]{:S(2)}, u32[]{:S(2)}) %collective-permute-start.2) | collective-permute-done | bytes 524320 | tf_op jit(solution)/shard_map/ppermute | solution.py:251
  97.6 2.6 %collective-permute-done.4.refs_3_ = bf16[256,1024]{1,0:T(8,128)(2,1)} collective-permute-done((bf16[256,1024]{1,0:T(8,128)(2,1)}, bf16[256,1024]{1,0:T(8,128)(2,1)}, u32[]{:S(2)}, u32[]{:S(2)}) %collective-permute-start.4) | collective-permute-done | bytes 524320 | tf_op jit(solution)/shard_map/ppermute | solution.py:251
  100.3 4.2 %project_out.2 = bf16[4,1024,128]{2,1,0:T(8,128)(2,1)} custom-call(s32[1]{0:T(128)} %bitcast.6.index, s32[1]{0:T(128)S(6)} %sub.3.side, bf16[256,1024]{1,0:T(8,128)(2,1)} %get-tuple-element.12.att.refs_0_, bf16[256,1024]{1,0:T(8,128)(2,1)} %copy-done.2, bf16[256,1024]{1,0:T(8,128)(2,1)} %copy-done.3, bf16[256,1024]{1,0:T(8,128)(2,1)} %collective-permute-done.4.refs_3_, ...), custom_call_target="tpu_custom_call" | custom-call | flops 1073741824 | bytes 4194304 | tf_op jit(solution)/shard_map/project_out/pallas_call | solution.py:215
  106.4 2.8 %collective-permute-done.5.refs_7_ = bf16[4,1024,128]{2,1,0:T(8,128)(2,1)S(1)} collective-permute-done((bf16[4,1024,128]{2,1,0:T(8,128)(2,1)}, bf16[4,1024,128]{2,1,0:T(8,128)(2,1)S(1)}, u32[]{:S(2)}, u32[]{:S(2)}) %collective-permute-start.5) | collective-permute-done | bytes 1048608 | tf_op jit(solution)/shard_map/ppermute | solution.py:245
  110.3 4.5 %project_out.3 = bf16[4,1024,128]{2,1,0:T(8,128)(2,1)} custom-call(s32[1]{0:T(128)} %bitcast.6.index, s32[1]{0:T(128)} %bitcast.7.side, bf16[256,1024]{1,0:T(8,128)(2,1)} %get-tuple-element.12.att.refs_0_, bf16[256,1024]{1,0:T(8,128)(2,1)} %copy-done.2, bf16[256,1024]{1,0:T(8,128)(2,1)} %copy-done.3, bf16[256,1024]{1,0:T(8,128)(2,1)} %collective-permute-done.4.refs_3_, ...), custom_call_target="tpu_custom_call" | custom-call | flops 1073741824 | bytes 4194304 | tf_op jit(solution)/shard_map/project_out/pallas_call | solution.py:215
  114.8 19.4 %all_to_all.32 = bf16[4,1024,128]{2,1,0:T(8,128)(2,1)S(1)} all-to-all(bf16[4,1024,128]{2,1,0:T(8,128)(2,1)} %project_out.3), channel_id=1, replica_groups=mesh['z_far'=8,'z_pair'=2,'x'=4,'y'=4,'core'=2] {'y'}, dimensions={0} | all-to-all | bytes 2097152 | tf_op jit(solution)/shard_map/all_to_all | solution.py:232
  134.2 3.9 %all-to-all-start.3 = ((bf16[4,256,1024]{2,1,0:T(8,128)(2,1)}), bf16[4,256,1024]{2,1,0:T(8,128)(2,1)S(1)}, u32[]{:S(2)}, u32[]{:S(2)}) async-start(bf16[4,256,1024]{2,1,0:T(8,128)(2,1)} %shard_map.93.refs_6_), calls=%async_computation.3 | async-start | bytes 4194304 | tf_op jit(solution)/shard_map/all_to_all | solution.py:232
  139.0 24.3 %all-to-all-done.3.d_parts = bf16[4,256,1024]{2,1,0:T(8,128)(2,1)S(1)} async-done(((bf16[4,256,1024]{2,1,0:T(8,128)(2,1)}), bf16[4,256,1024]{2,1,0:T(8,128)(2,1)S(1)}, u32[]{:S(2)}, u32[]{:S(2)}) %all-to-all-start.3) | async-done | bytes 2097184 | tf_op jit(solution)/shard_map/all_to_all | solution.py:232
  163.3 3.4 %all-to-all-start.5 = ((bf16[4,256,128]{2,1,0:T(8,128)(2,1)}), bf16[4,256,128]{2,1,0:T(8,128)(2,1)S(1)}, u32[]{:S(2)}, u32[]{:S(2)}) async-start(bf16[4,256,128]{2,1,0:T(8,128)(2,1)} %bitcast.8), calls=%async_computation.5 | async-start | bytes 524288 | tf_op jit(solution)/shard_map/all_to_all | solution.py:232
  166.7 8.0 %shard_map.95 = (bf16[256,1024]{1,0:T(8,128)(2,1)}, bf16[512,128]{1,0:T(8,128)(2,1)}, bf16[512,128]{1,0:T(8,128)(2,1)}, f32[512,128]{1,0:T(8,128)}) custom-call(bf16[256,1024]{1,0:T(8,128)(2,1)} %q.3, bf16[512,128]{1,0:T(8,128)(2,1)} %copy-done.9, bf16[512,128]{1,0:T(8,128)(2,1)} %copy-done.10, bf16[512,128]{1,0:T(8,128)(2,1)} %copy-done.8, ...), custom_call_target="tpu_custom_call" | custom-call | flops 8589934592 | bytes 8388608 | tf_op jit(solution)/shard_map/pallas_call | solution.py:144
  174.7 7.3 %collective-permute-start.7 = (bf16[512,128]{1,0:T(8,128)(2,1)}, bf16[512,128]{1,0:T(8,128)(2,1)S(1)}, u32[]{:S(2)}, u32[]{:S(2)}) collective-permute-start(bf16[512,128]{1,0:T(8,128)(2,1)} %get-tuple-element.19), channel_id=1, source_target_pairs={{8,0},{16,8},{24,16},{32,24},{40,32},{48,40},{56,48},{64,56},{72,6... | collective-permute-start | bytes 393224 | tf_op jit(solution)/shard_map/ppermute | solution.py:241
  182.1 2.8 %collective-permute-start.6 = (bf16[512,128]{1,0:T(8,128)(2,1)}, bf16[512,128]{1,0:T(8,128)(2,1)S(1)}, u32[]{:S(2)}, u32[]{:S(2)}) collective-permute-start(bf16[512,128]{1,0:T(8,128)(2,1)} %get-tuple-element.18), channel_id=1, source_target_pairs={{16,0},{24,8},{32,16},{40,24},{48,32},{56,40},{64,48},{72,56},{80,... | collective-permute-start | bytes 393224 | tf_op jit(solution)/shard_map/ppermute | solution.py:241
  185.0 5.6 %collective-permute-done.6 = bf16[512,128]{1,0:T(8,128)(2,1)S(1)} collective-permute-done((bf16[512,128]{1,0:T(8,128)(2,1)}, bf16[512,128]{1,0:T(8,128)(2,1)S(1)}, u32[]{:S(2)}, u32[]{:S(2)}) %collective-permute-start.6) | collective-permute-done | bytes 131104 | tf_op jit(solution)/shard_map/ppermute | solution.py:241
  (45 shorter events, 13.5 us)
Async XLA Ops:
  7.2 13.1 %copy-start.5 = (bf16[256,512]{1,0:T(8,128)(2,1)S(1)}, bf16[256,512]{1,0:T(8,128)(2,1)}, u32[]{:S(2)}) copy-start(bf16[256,512]{1,0:T(8,128)(2,1)} %param.9) | copy-start | bytes 786436
  7.2 71.7 %all-gather.2.cloned.1.call-start = ((), (), s32[]{:S(2)}) async-start(), calls=%async_computation.6 | async-start | bytes 2359296 | tf_op jit(solution)/shard_map/all_gather | solution.py:265
  31.3 4.6 %copy-start.6 = (bf16[256,128]{1,0:T(8,128)(2,1)S(1)}, bf16[256,128]{1,0:T(8,128)(2,1)}, u32[]{:S(2)}) copy-start(bf16[256,128]{1,0:T(8,128)(2,1)} %param.7) | copy-start | bytes 196612
  31.3 4.6 %copy-start.7 = (bf16[256,128]{1,0:T(8,128)(2,1)S(1)}, bf16[256,128]{1,0:T(8,128)(2,1)}, u32[]{:S(2)}) copy-start(bf16[256,128]{1,0:T(8,128)(2,1)} %param.8) | copy-start | bytes 196612
  31.3 47.2 %all-to-all-start.1 = ((bf16[8,1024,128]{2,1,0:T(8,128)(2,1)}), bf16[8,1024,128]{2,1,0:T(8,128)(2,1)S(1)}, u32[]{:S(2)}, u32[]{:S(2)}) async-start(bf16[8,1024,128]{2,1,0:T(8,128)(2,1)} %broadcast_in_dim.8), calls=%async_computation.1 | async-start | bytes 4194304 | tf_op jit(solution)/shard_map/all_to_all | solution.py:232
  35.9 25.1 %copy-start.8 = (bf16[512,128]{1,0:T(8,128)(2,1)}, bf16[512,128]{1,0:T(8,128)(2,1)S(1)}, u32[]{:S(2)}) copy-start(bf16[512,128]{1,0:T(8,128)(2,1)S(1)} %constant_dynamic-update-slice_fusion.k0.v0) | copy-start | bytes 393220
  35.9 17.0 %collective-permute-start = (bf16[512,128]{1,0:T(8,128)(2,1)S(1)}, bf16[512,128]{1,0:T(8,128)(2,1)S(1)}, u32[]{:S(2)}, u32[]{:S(2)}) collective-permute-start(bf16[512,128]{1,0:T(8,128)(2,1)S(1)} %constant_dynamic-update-slice_fusion.k0.v0), channel_id=1, source_target_pairs={{0,16},{8,24},{16,32},{24,40},{32,48},{40,56},{48,64},{56,72},{64,... | collective-permute-start | bytes 393224 | tf_op jit(solution)/shard_map/ppermute | solution.py:241
  38.7 22.4 %collective-permute-start.1 = (bf16[512,128]{1,0:T(8,128)(2,1)S(1)}, bf16[512,128]{1,0:T(8,128)(2,1)S(1)}, u32[]{:S(2)}, u32[]{:S(2)}) collective-permute-start(bf16[512,128]{1,0:T(8,128)(2,1)S(1)} %constant_dynamic-update-slice_fusion.k0.v0), channel_id=1, source_target_pairs={{0,8},{8,16},{16,24},{24,32},{32,40},{40,48},{48,56},{56,64},{64,7... | collective-permute-start | bytes 393224 | tf_op jit(solution)/shard_map/ppermute | solution.py:241
  52.9 8.1 %copy-start.9 = (bf16[512,128]{1,0:T(8,128)(2,1)}, bf16[512,128]{1,0:T(8,128)(2,1)S(1)}, u32[]{:S(2)}) copy-start(bf16[512,128]{1,0:T(8,128)(2,1)S(1)} %collective-permute-done.k2.v2) | copy-start | bytes 393220
  61.0 0.6 copy-start.10
  69.5 28.2 %collective-permute-start.2 = (bf16[256,1024]{1,0:T(8,128)(2,1)}, bf16[256,1024]{1,0:T(8,128)(2,1)S(1)}, u32[]{:S(2)}, u32[]{:S(2)}) collective-permute-start(bf16[256,1024]{1,0:T(8,128)(2,1)} %get-tuple-element.12.att.refs_0_), channel_id=1, source_target_pairs={{0,8},{8,16},{16,24},{24,0},{1,9},{9,17},{17,25},{25,1},{2,10},{10... | collective-permute-start | bytes 1572872 | tf_op jit(solution)/shard_map/ppermute | solution.py:251
  71.4 26.3 %collective-permute-start.3 = (bf16[256,1024]{1,0:T(8,128)(2,1)}, bf16[256,1024]{1,0:T(8,128)(2,1)S(1)}, u32[]{:S(2)}, u32[]{:S(2)}) collective-permute-start(bf16[256,1024]{1,0:T(8,128)(2,1)} %get-tuple-element.12.att.refs_0_), channel_id=1, source_target_pairs={{0,16},{8,24},{16,0},{24,8},{1,17},{9,25},{17,1},{25,9},{2,18},{10... | collective-permute-start | bytes 1572872 | tf_op jit(solution)/shard_map/ppermute | solution.py:251
  73.3 27.0 %collective-permute-start.4 = (bf16[256,1024]{1,0:T(8,128)(2,1)}, bf16[256,1024]{1,0:T(8,128)(2,1)}, u32[]{:S(2)}, u32[]{:S(2)}) collective-permute-start(bf16[256,1024]{1,0:T(8,128)(2,1)} %get-tuple-element.12.att.refs_0_), channel_id=1, source_target_pairs={{0,24},{8,0},{16,8},{24,16},{1,25},{9,1},{17,9},{25,17},{2,26},{10... | collective-permute-start | bytes 1572872 | tf_op jit(solution)/shard_map/ppermute | solution.py:251
  78.5 1.4 copy-start
  97.6 2.6 %copy-start.2 = (bf16[256,1024]{1,0:T(8,128)(2,1)}, bf16[256,1024]{1,0:T(8,128)(2,1)S(1)}, u32[]{:S(2)}) copy-start(bf16[256,1024]{1,0:T(8,128)(2,1)S(1)} %collective-permute-done.2.refs_1_) | copy-start | bytes 1572868
  97.6 2.6 %copy-start.3 = (bf16[256,1024]{1,0:T(8,128)(2,1)}, bf16[256,1024]{1,0:T(8,128)(2,1)S(1)}, u32[]{:S(2)}) copy-start(bf16[256,1024]{1,0:T(8,128)(2,1)S(1)} %collective-permute-done.3.refs_2_) | copy-start | bytes 1572868
  104.5 4.8 %collective-permute-start.5 = (bf16[4,1024,128]{2,1,0:T(8,128)(2,1)}, bf16[4,1024,128]{2,1,0:T(8,128)(2,1)S(1)}, u32[]{:S(2)}, u32[]{:S(2)}) collective-permute-start(bf16[4,1024,128]{2,1,0:T(8,128)(2,1)} %project_out.2), channel_id=1, source_target_pairs={{0,1},{1,0},{2,3},{3,2},{4,5},{5,4},{6,7},{7,6},{8,9},{9,8},{10,11... | collective-permute-start | bytes 3145736 | tf_op jit(solution)/shard_map/ppermute | solution.py:245
  109.2 1.1 copy-start.4
  134.2 29.1 %all-to-all-start.3 = ((bf16[4,256,1024]{2,1,0:T(8,128)(2,1)}), bf16[4,256,1024]{2,1,0:T(8,128)(2,1)S(1)}, u32[]{:S(2)}, u32[]{:S(2)}) async-start(bf16[4,256,1024]{2,1,0:T(8,128)(2,1)} %shard_map.93.refs_6_), calls=%async_computation.3 | async-start | bytes 4194304 | tf_op jit(solution)/shard_map/all_to_all | solution.py:232
  163.3 3.4 %copy-start.1 = (bf16[4,256,1024]{2,1,0:T(8,128)(2,1)}, bf16[4,256,1024]{2,1,0:T(8,128)(2,1)S(1)}, u32[]{:S(2)}) copy-start(bf16[4,256,1024]{2,1,0:T(8,128)(2,1)S(1)} %all-to-all-done.3.d_parts) | copy-start | bytes 6291460
  163.3 21.5 %all-to-all-start.5 = ((bf16[4,256,128]{2,1,0:T(8,128)(2,1)}), bf16[4,256,128]{2,1,0:T(8,128)(2,1)S(1)}, u32[]{:S(2)}, u32[]{:S(2)}) async-start(bf16[4,256,128]{2,1,0:T(8,128)(2,1)} %bitcast.8), calls=%async_computation.5 | async-start | bytes 524288 | tf_op jit(solution)/shard_map/all_to_all | solution.py:232
  174.7 10.3 %collective-permute-start.7 = (bf16[512,128]{1,0:T(8,128)(2,1)}, bf16[512,128]{1,0:T(8,128)(2,1)S(1)}, u32[]{:S(2)}, u32[]{:S(2)}) collective-permute-start(bf16[512,128]{1,0:T(8,128)(2,1)} %get-tuple-element.19), channel_id=1, source_target_pairs={{8,0},{16,8},{24,16},{32,24},{40,32},{48,40},{56,48},{64,56},{72,6... | collective-permute-start | bytes 393224 | tf_op jit(solution)/shard_map/ppermute | solution.py:241
  182.1 8.6 %collective-permute-start.6 = (bf16[512,128]{1,0:T(8,128)(2,1)}, bf16[512,128]{1,0:T(8,128)(2,1)S(1)}, u32[]{:S(2)}, u32[]{:S(2)}) collective-permute-start(bf16[512,128]{1,0:T(8,128)(2,1)} %get-tuple-element.18), channel_id=1, source_target_pairs={{16,0},{24,8},{32,16},{40,24},{48,32},{56,40},{64,48},{72,56},{80,... | collective-permute-start | bytes 393224 | tf_op jit(solution)/shard_map/ppermute | solution.py:241
Sparse Core Ops, SparseCore 0:
  20.4 58.4 all-gather.1

commit v2 on v1

--- a/solution.py
+++ b/solution.py
@@ -136,7 +136,7 @@
             to[rows:, :] = dva[own, :].astype(to.dtype)
 
 
-def backward(q, pairs, d_parts, att, shares, group=2):
+def backward(q, pairs, d_parts, att, shares, group=4):
     rows, width = q.shape
     heads = width // HD
     head = pl.BlockSpec((rows, group * HD), lambda i: (0, i))
@@ -276,9 +276,8 @@
     outward = project_out(index, 1 - core, attended_all, weight, d_here)
     outward = partner(outward, "core")
     projected = project_out(index, core, attended_all, weight, d_here, outward)
-    projected = swap(projected, "y")
-    projected = projected.astype(F32).sum(axis=0).astype(BF)
-    feature_parts = swap(projected.reshape(parts, rows, HD), "x")
+    projected = swap(projected.reshape(-1, rows, HD), ("y", "x"))
+    feature_parts = projected.reshape(-1, parts, rows, HD).astype(F32).sum(axis=0).astype(BF)
     query_grad, far2, far1, home = backward(queries, pairs, d_parts, attended, shares)
     two, one = shifted(far2, -2), shifted(far1, -1)
     home, feature_parts = lax.optimization_barrier((home, feature_parts))

time: 201 us -> 162 us (0.81)
  waiting for transfers between devices: 66.2 us -> 40.2 us
  blocking collectives: 40.4 us -> 20.9 us
  starting transfers between devices: 38.8 us -> 48.1 us
    all_to_all x3, waiting for transfers between devices: 24.3 us -> 4.66 us  [swap(): return lax.all_to_all(pieces, axis, 0, 0, tiled=True)]
    all_to_all x3 -> x2, blocking collectives: 40.4 us -> 20.9 us  [swap(): return lax.all_to_all(pieces, axis, 0, 0, tiled=True)]
    all_to_all x3, starting transfers between devices: 11.9 us -> 21.1 us  [swap(): return lax.all_to_all(pieces, axis, 0, 0, tiled=True)]
    ppermute x3, waiting for transfers between devices: 13.6 us -> 6.68 us  [around(): lax.ppermute(blocks[k], axis, [(i, (i + k * step) % size) for i in range(...]
  transfers between devices with their start and end apart: 12 -> 12, of which waited for: 9 -> 9; matrix products, arithmetic and copies ran while one was open for 1% -> 1% of each run, Pallas kernels for 11% -> 19%
where the time goes in v2:
time: 162 us; the launch traced here: 161 us
  starting transfers between devices  48.1 us (30%)
  waiting for transfers between devices  40.2 us (25%)
  Pallas kernels  30.3 us (19%)
  blocking collectives  20.9 us (13%)
  between operations  14.3 us (9%)
  local copies, waits for them, and re-layouts  5.62 us (3%)
  other arithmetic  1.97 us (1%)
    ppermute x4, waiting for transfers between devices, shifted(): lax.ppermute(block, DP, [(i, i + distance) for i in range(size) if 0 <= i...  24.8 us
    all_to_all x3, starting transfers between devices, swap(): return lax.all_to_all(pieces, axis, 0, 0, tiled=True)  21.1 us
    all_to_all x2, blocking collectives, swap(): return lax.all_to_all(pieces, axis, 0, 0, tiled=True)  20.9 us
    ppermute x4, starting transfers between devices, shifted(): lax.ppermute(block, DP, [(i, i + distance) for i in range(size) if 0 <= i...  16.1 us
    ppermute x3, starting transfers between devices, around(): lax.ppermute(blocks[k], axis, [(i, (i + k * step) % size) for i in range(...  8.97 us
    pallas_call x2, Pallas kernels, project_out(): pl.pallas_call(functools.partial(out_body, parts), grid_spec=pltpu.Prefet...  8.68 us
    pallas_call x1, Pallas kernels, forward(): call(functools.partial(forward_body, 1.0 / math.sqrt(HD), group), 8 << 30...  7.78 us
    pallas_call x1, Pallas kernels, backward(): call(functools.partial(backward_body, 1.0 / math.sqrt(HD), group), 8 << 3...  7.13 us
  transfers between devices with their start and end apart: 12, of which 9 were waited for; matrix products, arithmetic and copies ran while one was open for 1% of the time, Pallas kernels for 19%

profile of v2, /device:TPU:384, one launch (start us, length us, event | category | flops | bytes accessed | tf_op | source)
XLA Modules:
  0.0 161.4 jit_solution(5294578764223734737)
XLA Ops:
  8.4 11.9 %all_to_all.25 = bf16[8,16,1024]{2,1,0:T(8,128)(2,1)} all-to-all(bf16[8,16,1024]{2,1,0:T(8,128)(2,1)S(1)} %pad_maximum_fusion), channel_id=1, replica_groups=mesh['z_far'=8,'z_pair'=2,'x'=4,'y'=4,'core'=2] {'z_pair','x'}, dimensions={0} | all-to-all | bytes 524288 | tf_op jit(solution)/shard_map/all_to_all | solution.py:232
  20.6 9.1 %all_to_all.26 = bf16[4,256,128]{2,1,0:T(8,128)(2,1)S(1)} all-to-all(bf16[4,256,128]{2,1,0:T(8,128)(2,1)S(1)} %copy.14), channel_id=1, replica_groups=mesh['z_far'=8,'z_pair'=2,'x'=4,'y'=4,'core'=2] {'x'}, dimensions={0} | all-to-all | bytes 524288 | tf_op jit(solution)/shard_map/all_to_all | solution.py:232
  31.3 4.6 %all-to-all-start.1 = ((bf16[8,1024,128]{2,1,0:T(8,128)(2,1)}), bf16[8,1024,128]{2,1,0:T(8,128)(2,1)S(1)}, u32[]{:S(2)}, u32[]{:S(2)}) async-start(bf16[8,1024,128]{2,1,0:T(8,128)(2,1)} %broadcast_in_dim.8), calls=%async_computation.1 | async-start | bytes 4194304 | tf_op jit(solution)/shard_map/all_to_all | solution.py:232
  35.9 2.7 %collective-permute-start = (bf16[512,128]{1,0:T(8,128)(2,1)S(1)}, bf16[512,128]{1,0:T(8,128)(2,1)S(1)}, u32[]{:S(2)}, u32[]{:S(2)}) collective-permute-start(bf16[512,128]{1,0:T(8,128)(2,1)S(1)} %constant_dynamic-update-slice_fusion.k0.v0), channel_id=1, source_target_pairs={{0,16},{8,24},{16,32},{24,40},{32,48},{40,56},{48,64},{56,72},{64,... | collective-permute-start | bytes 393224 | tf_op jit(solution)/shard_map/ppermute | solution.py:241
  38.6 3.1 %collective-permute-start.1 = (bf16[512,128]{1,0:T(8,128)(2,1)S(1)}, bf16[512,128]{1,0:T(8,128)(2,1)S(1)}, u32[]{:S(2)}, u32[]{:S(2)}) collective-permute-start(bf16[512,128]{1,0:T(8,128)(2,1)S(1)} %constant_dynamic-update-slice_fusion.k0.v0), channel_id=1, source_target_pairs={{0,8},{8,16},{16,24},{24,32},{32,40},{40,48},{48,56},{56,64},{64,7... | collective-permute-start | bytes 393224 | tf_op jit(solution)/shard_map/ppermute | solution.py:241
  41.8 11.1 %collective-permute-done.k2.v2 = bf16[512,128]{1,0:T(8,128)(2,1)S(1)} collective-permute-done((bf16[512,128]{1,0:T(8,128)(2,1)S(1)}, bf16[512,128]{1,0:T(8,128)(2,1)S(1)}, u32[]{:S(2)}, u32[]{:S(2)}) %collective-permute-start) | collective-permute-done | bytes 131104 | tf_op jit(solution)/shard_map/ppermute | solution.py:241
  52.9 8.1 %collective-permute-done.1.k1.v1 = bf16[512,128]{1,0:T(8,128)(2,1)S(1)} collective-permute-done((bf16[512,128]{1,0:T(8,128)(2,1)S(1)}, bf16[512,128]{1,0:T(8,128)(2,1)S(1)}, u32[]{:S(2)}, u32[]{:S(2)}) %collective-permute-start.1) | collective-permute-done | bytes 131104 | tf_op jit(solution)/shard_map/ppermute | solution.py:241
  61.7 7.8 %shard_map.94 = (bf16[256,1024]{1,0:T(8,128)(2,1)}, bf16[8,768,256]{2,1,0:T(8,128)(2,1)}) custom-call(s32[64]{0:T(128)} %lengths.1, s32[1]{0:T(128)} %bitcast.5.place, bf16[256,1024]{1,0:T(8,128)(2,1)} %q.3, bf16[512,128]{1,0:T(8,128)(2,1)} %copy-done.7, bf16[512,128]{1,0:T(8,128)(2,1)} %copy-done.8, bf16[512,128]{1,0:T(8,128)(2,1)} %copy-done.6, ...), custom_call_target="tpu_custom_call" | custom-call | flops 8589934592 | bytes 8388608 | tf_op jit(solution)/shard_map/pallas_call | solution.py:86
  69.5 1.9 %collective-permute-start.2 = (bf16[256,1024]{1,0:T(8,128)(2,1)}, bf16[256,1024]{1,0:T(8,128)(2,1)}, u32[]{:S(2)}, u32[]{:S(2)}) collective-permute-start(bf16[256,1024]{1,0:T(8,128)(2,1)} %get-tuple-element.12.att.refs_0_), channel_id=1, source_target_pairs={{0,8},{8,16},{16,24},{24,0},{1,9},{9,17},{17,25},{25,1},{2,10},{10... | collective-permute-start | bytes 1572872 | tf_op jit(solution)/shard_map/ppermute | solution.py:251
  71.4 1.9 %collective-permute-start.3 = (bf16[256,1024]{1,0:T(8,128)(2,1)}, bf16[256,1024]{1,0:T(8,128)(2,1)}, u32[]{:S(2)}, u32[]{:S(2)}) collective-permute-start(bf16[256,1024]{1,0:T(8,128)(2,1)} %get-tuple-element.12.att.refs_0_), channel_id=1, source_target_pairs={{0,16},{8,24},{16,0},{24,8},{1,17},{9,25},{17,1},{25,9},{2,18},{10... | collective-permute-start | bytes 1572872 | tf_op jit(solution)/shard_map/ppermute | solution.py:251
  73.3 5.1 %collective-permute-start.4 = (bf16[256,1024]{1,0:T(8,128)(2,1)}, bf16[256,1024]{1,0:T(8,128)(2,1)}, u32[]{:S(2)}, u32[]{:S(2)}) collective-permute-start(bf16[256,1024]{1,0:T(8,128)(2,1)} %get-tuple-element.12.att.refs_0_), channel_id=1, source_target_pairs={{0,24},{8,0},{16,8},{24,16},{1,25},{9,1},{17,9},{25,17},{2,26},{10... | collective-permute-start | bytes 1572872 | tf_op jit(solution)/shard_map/ppermute | solution.py:251
  79.9 6.8 %shard_map.93.refs_6_ = bf16[4,256,1024]{2,1,0:T(8,128)(2,1)} custom-call(bf16[8,1024,128]{2,1,0:T(8,128)(2,1)} %copy-done, bf16[1024,1024]{1,0:T(8,128)(2,1)} %all-gather.2.cloned.1.call-done.w.refs_4_.refs_5_), custom_call_target="tpu_custom_call" | custom-call | flops 2147483648 | bytes 8388608 | tf_op jit(solution)/shard_map/pallas_call | solution.py:179
  86.6 8.4 %all-to-all-start.3 = ((bf16[4,256,1024]{2,1,0:T(8,128)(2,1)}), bf16[4,256,1024]{2,1,0:T(8,128)(2,1)S(1)}, u32[]{:S(2)}, u32[]{:S(2)}) async-start(bf16[4,256,1024]{2,1,0:T(8,128)(2,1)} %shard_map.93.refs_6_), calls=%async_computation.3 | async-start | bytes 4194304 | tf_op jit(solution)/shard_map/all_to_all | solution.py:232
  95.1 2.7 %collective-permute-done.2.refs_1_ = bf16[256,1024]{1,0:T(8,128)(2,1)} collective-permute-done((bf16[256,1024]{1,0:T(8,128)(2,1)}, bf16[256,1024]{1,0:T(8,128)(2,1)}, u32[]{:S(2)}, u32[]{:S(2)}) %collective-permute-start.2) | collective-permute-done | bytes 524320 | tf_op jit(solution)/shard_map/ppermute | solution.py:251
  97.7 4.0 %collective-permute-done.4.refs_3_ = bf16[256,1024]{1,0:T(8,128)(2,1)} collective-permute-done((bf16[256,1024]{1,0:T(8,128)(2,1)}, bf16[256,1024]{1,0:T(8,128)(2,1)}, u32[]{:S(2)}, u32[]{:S(2)}) %collective-permute-start.4) | collective-permute-done | bytes 524320 | tf_op jit(solution)/shard_map/ppermute | solution.py:251
  101.7 4.2 %project_out.2 = bf16[4,1024,128]{2,1,0:T(8,128)(2,1)} custom-call(s32[1]{0:T(128)} %bitcast.6.index, s32[1]{0:T(128)S(6)} %sub.3.side, bf16[256,1024]{1,0:T(8,128)(2,1)} %get-tuple-element.12.att.refs_0_, bf16[256,1024]{1,0:T(8,128)(2,1)} %collective-permute-done.2.refs_1_, bf16[256,1024]{1,0:T(8,128)(2,1)} %collective-permute-done.3.refs_2_, ...), custom_call_target="tpu_custom_call" | custom-call | flops 1073741824 | bytes 4194304 | tf_op jit(solution)/shard_map/project_out/pallas_call | solution.py:215
  107.8 2.8 %collective-permute-done.5.refs_7_ = bf16[4,1024,128]{2,1,0:T(8,128)(2,1)S(1)} collective-permute-done((bf16[4,1024,128]{2,1,0:T(8,128)(2,1)}, bf16[4,1024,128]{2,1,0:T(8,128)(2,1)S(1)}, u32[]{:S(2)}, u32[]{:S(2)}) %collective-permute-start.5) | collective-permute-done | bytes 1048608 | tf_op jit(solution)/shard_map/ppermute | solution.py:245
  111.7 4.5 %project_out.3 = bf16[4,1024,128]{2,1,0:T(8,128)(2,1)} custom-call(s32[1]{0:T(128)} %bitcast.6.index, s32[1]{0:T(128)} %bitcast.7.side, bf16[256,1024]{1,0:T(8,128)(2,1)} %get-tuple-element.12.att.refs_0_, bf16[256,1024]{1,0:T(8,128)(2,1)} %collective-permute-done.2.refs_1_, bf16[256,1024]{1,0:T(8,128)(2,1)} %collective-permute-done.3.refs_2_, ...), custom_call_target="tpu_custom_call" | custom-call | flops 1073741824 | bytes 4194304 | tf_op jit(solution)/shard_map/project_out/pallas_call | solution.py:215
  116.2 4.7 %all-to-all-done.3.d_parts = bf16[4,256,1024]{2,1,0:T(8,128)(2,1)S(1)} async-done(((bf16[4,256,1024]{2,1,0:T(8,128)(2,1)}), bf16[4,256,1024]{2,1,0:T(8,128)(2,1)S(1)}, u32[]{:S(2)}, u32[]{:S(2)}) %all-to-all-start.3) | async-done | bytes 2097184 | tf_op jit(solution)/shard_map/all_to_all | solution.py:232
  120.9 8.0 %all-to-all-start.4 = ((bf16[16,256,128]{2,1,0:T(8,128)(2,1)}), bf16[16,256,128]{2,1,0:T(8,128)(2,1)S(1)}, u32[]{:S(2)}, u32[]{:S(2)}) async-start(bf16[16,256,128]{2,1,0:T(8,128)(2,1)} %bitcast.22), calls=%async_computation.4 | async-start | bytes 2097152 | tf_op jit(solution)/shard_map/all_to_all | solution.py:232
  129.0 7.1 %shard_map.95 = (bf16[256,1024]{1,0:T(8,128)(2,1)}, bf16[512,128]{1,0:T(8,128)(2,1)}, bf16[512,128]{1,0:T(8,128)(2,1)}, f32[512,128]{1,0:T(8,128)}) custom-call(bf16[256,1024]{1,0:T(8,128)(2,1)} %q.3, bf16[512,128]{1,0:T(8,128)(2,1)} %copy-done.7, bf16[512,128]{1,0:T(8,128)(2,1)} %copy-done.8, bf16[512,128]{1,0:T(8,128)(2,1)} %copy-done.6, ...), custom_call_target="tpu_custom_call" | custom-call | flops 8589934592 | bytes 8388608 | tf_op jit(solution)/shard_map/pallas_call | solution.py:144
  136.1 7.5 %collective-permute-start.7 = (bf16[512,128]{1,0:T(8,128)(2,1)}, bf16[512,128]{1,0:T(8,128)(2,1)S(1)}, u32[]{:S(2)}, u32[]{:S(2)}) collective-permute-start(bf16[512,128]{1,0:T(8,128)(2,1)} %get-tuple-element.19), channel_id=1, source_target_pairs={{8,0},{16,8},{24,16},{32,24},{40,32},{48,40},{56,48},{64,56},{72,6... | collective-permute-start | bytes 393224 | tf_op jit(solution)/shard_map/ppermute | solution.py:241
  143.6 2.8 %collective-permute-start.6 = (bf16[512,128]{1,0:T(8,128)(2,1)}, bf16[512,128]{1,0:T(8,128)(2,1)S(1)}, u32[]{:S(2)}, u32[]{:S(2)}) collective-permute-start(bf16[512,128]{1,0:T(8,128)(2,1)} %get-tuple-element.18), channel_id=1, source_target_pairs={{16,0},{24,8},{32,16},{40,24},{48,32},{56,40},{64,48},{72,56},{80,... | collective-permute-start | bytes 393224 | tf_op jit(solution)/shard_map/ppermute | solution.py:241
  147.4 4.8 %collective-permute-done.6 = bf16[512,128]{1,0:T(8,128)(2,1)S(1)} collective-permute-done((bf16[512,128]{1,0:T(8,128)(2,1)}, bf16[512,128]{1,0:T(8,128)(2,1)S(1)}, u32[]{:S(2)}, u32[]{:S(2)}) %collective-permute-start.6) | collective-permute-done | bytes 131104 | tf_op jit(solution)/shard_map/ppermute | solution.py:241
  (40 shorter events, 11.5 us)
Async XLA Ops:
  7.2 13.1 %copy-start.3 = (bf16[256,512]{1,0:T(8,128)(2,1)S(1)}, bf16[256,512]{1,0:T(8,128)(2,1)}, u32[]{:S(2)}) copy-start(bf16[256,512]{1,0:T(8,128)(2,1)} %param.9) | copy-start | bytes 786436
  7.2 72.5 %all-gather.2.cloned.1.call-start = ((), (), s32[]{:S(2)}) async-start(), calls=%async_computation.5 | async-start | bytes 2359296 | tf_op jit(solution)/shard_map/all_gather | solution.py:265
  31.2 4.6 %copy-start.4 = (bf16[256,128]{1,0:T(8,128)(2,1)S(1)}, bf16[256,128]{1,0:T(8,128)(2,1)}, u32[]{:S(2)}) copy-start(bf16[256,128]{1,0:T(8,128)(2,1)} %param.7) | copy-start | bytes 196612
  31.2 4.6 %copy-start.5 = (bf16[256,128]{1,0:T(8,128)(2,1)S(1)}, bf16[256,128]{1,0:T(8,128)(2,1)}, u32[]{:S(2)}) copy-start(bf16[256,128]{1,0:T(8,128)(2,1)} %param.8) | copy-start | bytes 196612
  31.3 47.2 %all-to-all-start.1 = ((bf16[8,1024,128]{2,1,0:T(8,128)(2,1)}), bf16[8,1024,128]{2,1,0:T(8,128)(2,1)S(1)}, u32[]{:S(2)}, u32[]{:S(2)}) async-start(bf16[8,1024,128]{2,1,0:T(8,128)(2,1)} %broadcast_in_dim.8), calls=%async_computation.1 | async-start | bytes 4194304 | tf_op jit(solution)/shard_map/all_to_all | solution.py:232
  35.9 25.1 %copy-start.6 = (bf16[512,128]{1,0:T(8,128)(2,1)}, bf16[512,128]{1,0:T(8,128)(2,1)S(1)}, u32[]{:S(2)}) copy-start(bf16[512,128]{1,0:T(8,128)(2,1)S(1)} %constant_dynamic-update-slice_fusion.k0.v0) | copy-start | bytes 393220
  35.9 17.0 %collective-permute-start = (bf16[512,128]{1,0:T(8,128)(2,1)S(1)}, bf16[512,128]{1,0:T(8,128)(2,1)S(1)}, u32[]{:S(2)}, u32[]{:S(2)}) collective-permute-start(bf16[512,128]{1,0:T(8,128)(2,1)S(1)} %constant_dynamic-update-slice_fusion.k0.v0), channel_id=1, source_target_pairs={{0,16},{8,24},{16,32},{24,40},{32,48},{40,56},{48,64},{56,72},{64,... | collective-permute-start | bytes 393224 | tf_op jit(solution)/shard_map/ppermute | solution.py:241
  38.6 22.4 %collective-permute-start.1 = (bf16[512,128]{1,0:T(8,128)(2,1)S(1)}, bf16[512,128]{1,0:T(8,128)(2,1)S(1)}, u32[]{:S(2)}, u32[]{:S(2)}) collective-permute-start(bf16[512,128]{1,0:T(8,128)(2,1)S(1)} %constant_dynamic-update-slice_fusion.k0.v0), channel_id=1, source_target_pairs={{0,8},{8,16},{16,24},{24,32},{32,40},{40,48},{48,56},{56,64},{64,7... | collective-permute-start | bytes 393224 | tf_op jit(solution)/shard_map/ppermute | solution.py:241
  52.9 8.1 %copy-start.7 = (bf16[512,128]{1,0:T(8,128)(2,1)}, bf16[512,128]{1,0:T(8,128)(2,1)S(1)}, u32[]{:S(2)}) copy-start(bf16[512,128]{1,0:T(8,128)(2,1)S(1)} %collective-permute-done.k2.v2) | copy-start | bytes 393220
  61.0 0.7 copy-start.8
  69.5 28.3 %collective-permute-start.2 = (bf16[256,1024]{1,0:T(8,128)(2,1)}, bf16[256,1024]{1,0:T(8,128)(2,1)}, u32[]{:S(2)}, u32[]{:S(2)}) collective-permute-start(bf16[256,1024]{1,0:T(8,128)(2,1)} %get-tuple-element.12.att.refs_0_), channel_id=1, source_target_pairs={{0,8},{8,16},{16,24},{24,0},{1,9},{9,17},{17,25},{25,1},{2,10},{10... | collective-permute-start | bytes 1572872 | tf_op jit(solution)/shard_map/ppermute | solution.py:251
  71.4 26.4 %collective-permute-start.3 = (bf16[256,1024]{1,0:T(8,128)(2,1)}, bf16[256,1024]{1,0:T(8,128)(2,1)}, u32[]{:S(2)}, u32[]{:S(2)}) collective-permute-start(bf16[256,1024]{1,0:T(8,128)(2,1)} %get-tuple-element.12.att.refs_0_), channel_id=1, source_target_pairs={{0,16},{8,24},{16,0},{24,8},{1,17},{9,25},{17,1},{25,9},{2,18},{10... | collective-permute-start | bytes 1572872 | tf_op jit(solution)/shard_map/ppermute | solution.py:251
  73.3 28.4 %collective-permute-start.4 = (bf16[256,1024]{1,0:T(8,128)(2,1)}, bf16[256,1024]{1,0:T(8,128)(2,1)}, u32[]{:S(2)}, u32[]{:S(2)}) collective-permute-start(bf16[256,1024]{1,0:T(8,128)(2,1)} %get-tuple-element.12.att.refs_0_), channel_id=1, source_target_pairs={{0,24},{8,0},{16,8},{24,16},{1,25},{9,1},{17,9},{25,17},{2,26},{10... | collective-permute-start | bytes 1572872 | tf_op jit(solution)/shard_map/ppermute | solution.py:251
  78.5 1.4 copy-start
  86.6 34.2 %all-to-all-start.3 = ((bf16[4,256,1024]{2,1,0:T(8,128)(2,1)}), bf16[4,256,1024]{2,1,0:T(8,128)(2,1)S(1)}, u32[]{:S(2)}, u32[]{:S(2)}) async-start(bf16[4,256,1024]{2,1,0:T(8,128)(2,1)} %shard_map.93.refs_6_), calls=%async_computation.3 | async-start | bytes 4194304 | tf_op jit(solution)/shard_map/all_to_all | solution.py:232
  105.9 4.8 %collective-permute-start.5 = (bf16[4,1024,128]{2,1,0:T(8,128)(2,1)}, bf16[4,1024,128]{2,1,0:T(8,128)(2,1)S(1)}, u32[]{:S(2)}, u32[]{:S(2)}) collective-permute-start(bf16[4,1024,128]{2,1,0:T(8,128)(2,1)} %project_out.2), channel_id=1, source_target_pairs={{0,1},{1,0},{2,3},{3,2},{4,5},{5,4},{6,7},{7,6},{8,9},{9,8},{10,11... | collective-permute-start | bytes 3145736 | tf_op jit(solution)/shard_map/ppermute | solution.py:245
  110.7 1.1 copy-start.2
  120.9 8.1 %copy-start.1 = (bf16[4,256,1024]{2,1,0:T(8,128)(2,1)}, bf16[4,256,1024]{2,1,0:T(8,128)(2,1)S(1)}, u32[]{:S(2)}) copy-start(bf16[4,256,1024]{2,1,0:T(8,128)(2,1)S(1)} %all-to-all-done.3.d_parts) | copy-start | bytes 6291460
  120.9 25.5 %all-to-all-start.4 = ((bf16[16,256,128]{2,1,0:T(8,128)(2,1)}), bf16[16,256,128]{2,1,0:T(8,128)(2,1)S(1)}, u32[]{:S(2)}, u32[]{:S(2)}) async-start(bf16[16,256,128]{2,1,0:T(8,128)(2,1)} %bitcast.22), calls=%async_computation.4 | async-start | bytes 2097152 | tf_op jit(solution)/shard_map/all_to_all | solution.py:232
  136.1 11.3 %collective-permute-start.7 = (bf16[512,128]{1,0:T(8,128)(2,1)}, bf16[512,128]{1,0:T(8,128)(2,1)S(1)}, u32[]{:S(2)}, u32[]{:S(2)}) collective-permute-start(bf16[512,128]{1,0:T(8,128)(2,1)} %get-tuple-element.19), channel_id=1, source_target_pairs={{8,0},{16,8},{24,16},{32,24},{40,32},{48,40},{56,48},{64,56},{72,6... | collective-permute-start | bytes 393224 | tf_op jit(solution)/shard_map/ppermute | solution.py:241
  143.6 8.6 %collective-permute-start.6 = (bf16[512,128]{1,0:T(8,128)(2,1)}, bf16[512,128]{1,0:T(8,128)(2,1)S(1)}, u32[]{:S(2)}, u32[]{:S(2)}) collective-permute-start(bf16[512,128]{1,0:T(8,128)(2,1)} %get-tuple-element.18), channel_id=1, source_target_pairs={{16,0},{24,8},{32,16},{40,24},{48,32},{56,40},{64,48},{72,56},{80,... | collective-permute-start | bytes 393224 | tf_op jit(solution)/shard_map/ppermute | solution.py:241
Sparse Core Ops, SparseCore 0:
  20.4 59.2 all-gather.1

commit v3 on v2

--- a/solution.py
+++ b/solution.py
@@ -160,31 +160,25 @@
     )(q, *pairs, *pairs, d_parts, att, shares)
 
 
-def back_body(og, w, out, lhs):
-    @pl.when(pl.program_id(0) == 0)
-    def _():
-        for h in range(og.shape[0]):
-            lhs[:, h * HD : (h + 1) * HD] = og[h]
-
+def back_body(cot, w, out):
     rows = out.shape[1]
-    done = dot_nt(lhs[...], w[...]).astype(BF)
+    done = dot_nt(cot[...], w[...]).astype(BF)
     for b in range(out.shape[0]):
         out[b] = done[b * rows : (b + 1) * rows]
 
 
-def project_back(og, w, parts, block=256):
-    _, tokens, _ = og.shape
-    inner, columns = w.shape
+def project_back(cot, w, parts, block=256):
+    tokens, columns = cot.shape
+    inner = w.shape[0]
     rows = tokens // parts
     return call(
         back_body,
         2 << 30,
         grid=(inner // block,),
-        in_specs=[pl.BlockSpec(memory_space=pltpu.VMEM), pl.BlockSpec((block, columns), lambda i: (i, 0))],
+        in_specs=[pl.BlockSpec((tokens, columns), lambda i: (0, 0)), pl.BlockSpec((block, columns), lambda i: (i, 0))],
         out_specs=pl.BlockSpec((parts, rows, block), lambda i: (0, 0, i)),
         out_shape=jax.ShapeDtypeStruct((parts, rows, inner), BF),
-        scratch_shapes=[pltpu.VMEM((tokens, columns), BF)],
-    )(og, w)
+    )(cot, w)
 
 
 def out_body(parts, index, side, *refs):
@@ -267,7 +261,7 @@
     pairs = [shifted(pair, 2), shifted(pair, 1), pair]
     own_g = output_grad.reshape(rows, parts, HD).transpose(1, 0, 2)
     grads = swap(own_g, "x").reshape(parts * rows, HD)
-    grads = everywhere(grads, HEAD)
+    grads = everywhere(grads, HEAD).transpose(1, 0, 2).reshape(parts * rows, HEADS * HD)
     attended, shares = forward(lengths, place, queries, pairs)
     attended_all = around([attended] * parts, "x", 1)
 
@@ -280,10 +274,12 @@
     feature_parts = projected.reshape(-1, parts, rows, HD).astype(F32).sum(axis=0).astype(BF)
     query_grad, far2, far1, home = backward(queries, pairs, d_parts, attended, shares)
     two, one = shifted(far2, -2), shifted(far1, -1)
-    home, feature_parts = lax.optimization_barrier((home, feature_parts))
     layer_out = jnp.concatenate([feature_parts[j] for j in range(parts)], axis=1)
-    total = (home + two.astype(F32) + one.astype(F32)).astype(BF)
-    return layer_out, query_grad, total[:rows], total[rows:]
+    home, layer_out = lax.optimization_barrier((home, layer_out))
+    key_grad, value_grad = [
+        (home[at] + two[at].astype(F32) + one[at].astype(F32)).astype(BF) for at in (slice(0, rows), slice(rows, None))
+    ]
+    return layer_out, query_grad, key_grad, value_grad
 
 
 def solution(mesh):

time: 162 us -> 160 us (0.988)
  waiting for transfers between devices: 40.2 us -> 38.4 us
    reshape x0 -> x1, local copies, waits for them, and re-layouts: none -> 1.73 us  [on_device(): everywhere(grads, HEAD).transpose(1, 0, 2).reshape(parts * rows, HEADS * HD)]
  transfers between devices with their start and end apart: 12 -> 12, of which waited for: 9 -> 7; matrix products, arithmetic and copies ran while one was open for 1% -> 3% of each run, Pallas kernels for 19% -> 19%
where the time goes in v3:
time: 160 us
  starting transfers between devices  48.1 us (30%)
  waiting for transfers between devices  38.4 us (24%)
  Pallas kernels  29.8 us (19%)
  blocking collectives  20.9 us (13%)
  between operations  14.3 us (9%)
  local copies, waits for them, and re-layouts  6.5 us (4%)
  other arithmetic  1.68 us (1%)
    ppermute x4, waiting for transfers between devices, shifted(): lax.ppermute(block, DP, [(i, i + distance) for i in range(size) if 0 <= i...  24.1 us
    all_to_all x3, starting transfers between devices, swap(): return lax.all_to_all(pieces, axis, 0, 0, tiled=True)  21.1 us
    all_to_all x2, blocking collectives, swap(): return lax.all_to_all(pieces, axis, 0, 0, tiled=True)  20.9 us
    ppermute x4, starting transfers between devices, shifted(): lax.ppermute(block, DP, [(i, i + distance) for i in range(size) if 0 <= i...  16.1 us
    ppermute x3, starting transfers between devices, around(): lax.ppermute(blocks[k], axis, [(i, (i + k * step) % size) for i in range(...  8.97 us
    pallas_call x2, Pallas kernels, project_out(): pl.pallas_call(functools.partial(out_body, parts), grid_spec=pltpu.Prefet...  8.68 us
    pallas_call x1, Pallas kernels, forward(): call(functools.partial(forward_body, 1.0 / math.sqrt(HD), group), 8 << 30...  7.78 us
    ppermute x3, waiting for transfers between devices, around(): lax.ppermute(blocks[k], axis, [(i, (i + k * step) % size) for i in range(...  7.3 us
  transfers between devices with their start and end apart: 12, of which 7 were waited for; matrix products, arithmetic and copies ran while one was open for 3% of the time, Pallas kernels for 19%

profile of v3, /device:TPU:384, one launch (start us, length us, event | category | flops | bytes accessed | tf_op | source)
XLA Modules:
  0.0 159.7 jit_solution(14257494443377550879)
XLA Ops:
  8.4 11.9 %all_to_all.25 = bf16[8,16,1024]{2,1,0:T(8,128)(2,1)} all-to-all(bf16[8,16,1024]{2,1,0:T(8,128)(2,1)S(1)} %pad_maximum_fusion), channel_id=1, replica_groups=mesh['z_far'=8,'z_pair'=2,'x'=4,'y'=4,'core'=2] {'z_pair','x'}, dimensions={0} | all-to-all | bytes 524288 | tf_op jit(solution)/shard_map/all_to_all | solution.py:226
  20.4 9.1 %all_to_all.26 = bf16[4,256,128]{1,2,0:T(8,128)(2,1)S(1)} all-to-all(bf16[4,256,128]{1,2,0:T(8,128)(2,1)S(1)} %bitcast.31), channel_id=1, replica_groups=mesh['z_far'=8,'z_pair'=2,'x'=4,'y'=4,'core'=2] {'x'}, dimensions={0} | all-to-all | bytes 524288 | tf_op jit(solution)/shard_map/all_to_all | solution.py:226
  31.3 4.6 %all-to-all-start.1 = ((bf16[8,1024,128]{2,1,0:T(8,128)(2,1)}), bf16[8,1024,128]{2,1,0:T(8,128)(2,1)S(1)}, u32[]{:S(2)}, u32[]{:S(2)}) async-start(bf16[8,1024,128]{2,1,0:T(8,128)(2,1)} %broadcast_in_dim.8), calls=%async_computation.1 | async-start | bytes 4194304 | tf_op jit(solution)/shard_map/all_to_all | solution.py:226
  35.9 2.7 %collective-permute-start = (bf16[512,128]{1,0:T(8,128)(2,1)S(1)}, bf16[512,128]{1,0:T(8,128)(2,1)S(1)}, u32[]{:S(2)}, u32[]{:S(2)}) collective-permute-start(bf16[512,128]{1,0:T(8,128)(2,1)S(1)} %constant_dynamic-update-slice_fusion.k0.v0), channel_id=1, source_target_pairs={{0,16},{8,24},{16,32},{24,40},{32,48},{40,56},{48,64},{56,72},{64,... | collective-permute-start | bytes 393224 | tf_op jit(solution)/shard_map/ppermute | solution.py:235
  38.7 3.1 %collective-permute-start.1 = (bf16[512,128]{1,0:T(8,128)(2,1)S(1)}, bf16[512,128]{1,0:T(8,128)(2,1)S(1)}, u32[]{:S(2)}, u32[]{:S(2)}) collective-permute-start(bf16[512,128]{1,0:T(8,128)(2,1)S(1)} %constant_dynamic-update-slice_fusion.k0.v0), channel_id=1, source_target_pairs={{0,8},{8,16},{16,24},{24,32},{32,40},{40,48},{48,56},{56,64},{64,7... | collective-permute-start | bytes 393224 | tf_op jit(solution)/shard_map/ppermute | solution.py:235
  41.8 11.1 %collective-permute-done.k2.v2 = bf16[512,128]{1,0:T(8,128)(2,1)S(1)} collective-permute-done((bf16[512,128]{1,0:T(8,128)(2,1)S(1)}, bf16[512,128]{1,0:T(8,128)(2,1)S(1)}, u32[]{:S(2)}, u32[]{:S(2)}) %collective-permute-start) | collective-permute-done | bytes 131104 | tf_op jit(solution)/shard_map/ppermute | solution.py:235
  52.9 8.1 %collective-permute-done.1.k1.v1 = bf16[512,128]{1,0:T(8,128)(2,1)S(1)} collective-permute-done((bf16[512,128]{1,0:T(8,128)(2,1)S(1)}, bf16[512,128]{1,0:T(8,128)(2,1)S(1)}, u32[]{:S(2)}, u32[]{:S(2)}) %collective-permute-start.1) | collective-permute-done | bytes 131104 | tf_op jit(solution)/shard_map/ppermute | solution.py:235
  61.7 7.8 %shard_map.94 = (bf16[256,1024]{1,0:T(8,128)(2,1)}, bf16[8,768,256]{2,1,0:T(8,128)(2,1)}) custom-call(s32[64]{0:T(128)} %lengths.1, s32[1]{0:T(128)} %bitcast.6.place, bf16[256,1024]{1,0:T(8,128)(2,1)} %q.3, bf16[512,128]{1,0:T(8,128)(2,1)} %copy-done.7, bf16[512,128]{1,0:T(8,128)(2,1)} %copy-done.8, bf16[512,128]{1,0:T(8,128)(2,1)} %copy-done.6, ...), custom_call_target="tpu_custom_call" | custom-call | flops 8589934592 | bytes 8388608 | tf_op jit(solution)/shard_map/pallas_call | solution.py:86
  69.5 1.9 %collective-permute-start.2 = (bf16[256,1024]{1,0:T(8,128)(2,1)}, bf16[256,1024]{1,0:T(8,128)(2,1)}, u32[]{:S(2)}, u32[]{:S(2)}) collective-permute-start(bf16[256,1024]{1,0:T(8,128)(2,1)} %get-tuple-element.12.att.refs_0_), channel_id=1, source_target_pairs={{0,8},{8,16},{16,24},{24,0},{1,9},{9,17},{17,25},{25,1},{2,10},{10... | collective-permute-start | bytes 1572872 | tf_op jit(solution)/shard_map/ppermute | solution.py:245
  71.4 1.9 %collective-permute-start.3 = (bf16[256,1024]{1,0:T(8,128)(2,1)}, bf16[256,1024]{1,0:T(8,128)(2,1)}, u32[]{:S(2)}, u32[]{:S(2)}) collective-permute-start(bf16[256,1024]{1,0:T(8,128)(2,1)} %get-tuple-element.12.att.refs_0_), channel_id=1, source_target_pairs={{0,16},{8,24},{16,0},{24,8},{1,17},{9,25},{17,1},{25,9},{2,18},{10... | collective-permute-start | bytes 1572872 | tf_op jit(solution)/shard_map/ppermute | solution.py:245
  73.3 5.1 %collective-permute-start.4 = (bf16[256,1024]{1,0:T(8,128)(2,1)}, bf16[256,1024]{1,0:T(8,128)(2,1)}, u32[]{:S(2)}, u32[]{:S(2)}) collective-permute-start(bf16[256,1024]{1,0:T(8,128)(2,1)} %get-tuple-element.12.att.refs_0_), channel_id=1, source_target_pairs={{0,24},{8,0},{16,8},{24,16},{1,25},{9,1},{17,9},{25,17},{2,26},{10... | collective-permute-start | bytes 1572872 | tf_op jit(solution)/shard_map/ppermute | solution.py:245
  80.2 6.2 %shard_map.93.refs_6_ = bf16[4,256,1024]{2,1,0:T(8,128)(2,1)} custom-call(bf16[1024,1024]{1,0:T(8,128)(2,1)} %copy_bitcast_fusion.cot, bf16[1024,1024]{1,0:T(8,128)(2,1)} %all-gather.2.cloned.1.call-done.w.refs_4_.refs_5_), custom_call_target="tpu_custom_call" | custom-call | flops 2147483648 | bytes 8388608 | tf_op jit(solution)/shard_map/pallas_call | solution.py:174
  86.4 8.1 %all-to-all-start.3 = ((bf16[4,256,1024]{2,1,0:T(8,128)(2,1)}), bf16[4,256,1024]{2,1,0:T(8,128)(2,1)S(1)}, u32[]{:S(2)}, u32[]{:S(2)}) async-start(bf16[4,256,1024]{2,1,0:T(8,128)(2,1)} %shard_map.93.refs_6_), calls=%async_computation.3 | async-start | bytes 4194304 | tf_op jit(solution)/shard_map/all_to_all | solution.py:226
  94.4 3.3 %collective-permute-done.2.refs_1_ = bf16[256,1024]{1,0:T(8,128)(2,1)} collective-permute-done((bf16[256,1024]{1,0:T(8,128)(2,1)}, bf16[256,1024]{1,0:T(8,128)(2,1)}, u32[]{:S(2)}, u32[]{:S(2)}) %collective-permute-start.2) | collective-permute-done | bytes 524320 | tf_op jit(solution)/shard_map/ppermute | solution.py:245
  97.7 4.0 %collective-permute-done.4.refs_3_ = bf16[256,1024]{1,0:T(8,128)(2,1)} collective-permute-done((bf16[256,1024]{1,0:T(8,128)(2,1)}, bf16[256,1024]{1,0:T(8,128)(2,1)}, u32[]{:S(2)}, u32[]{:S(2)}) %collective-permute-start.4) | collective-permute-done | bytes 524320 | tf_op jit(solution)/shard_map/ppermute | solution.py:245
  101.7 4.2 %project_out.2 = bf16[4,1024,128]{2,1,0:T(8,128)(2,1)} custom-call(s32[1]{0:T(128)} %bitcast.7.index, s32[1]{0:T(128)S(6)} %sub.3.side, bf16[256,1024]{1,0:T(8,128)(2,1)} %get-tuple-element.12.att.refs_0_, bf16[256,1024]{1,0:T(8,128)(2,1)} %collective-permute-done.2.refs_1_, bf16[256,1024]{1,0:T(8,128)(2,1)} %collective-permute-done.3.refs_2_, ...), custom_call_target="tpu_custom_call" | custom-call | flops 1073741824 | bytes 4194304 | tf_op jit(solution)/shard_map/project_out/pallas_call | solution.py:209
  107.8 2.8 %collective-permute-done.5.refs_7_ = bf16[4,1024,128]{2,1,0:T(8,128)(2,1)S(1)} collective-permute-done((bf16[4,1024,128]{2,1,0:T(8,128)(2,1)}, bf16[4,1024,128]{2,1,0:T(8,128)(2,1)S(1)}, u32[]{:S(2)}, u32[]{:S(2)}) %collective-permute-start.5) | collective-permute-done | bytes 1048608 | tf_op jit(solution)/shard_map/ppermute | solution.py:239
  111.7 4.5 %project_out.3 = bf16[4,1024,128]{2,1,0:T(8,128)(2,1)} custom-call(s32[1]{0:T(128)} %bitcast.7.index, s32[1]{0:T(128)} %bitcast.8.side, bf16[256,1024]{1,0:T(8,128)(2,1)} %get-tuple-element.12.att.refs_0_, bf16[256,1024]{1,0:T(8,128)(2,1)} %collective-permute-done.2.refs_1_, bf16[256,1024]{1,0:T(8,128)(2,1)} %collective-permute-done.3.refs_2_, ...), custom_call_target="tpu_custom_call" | custom-call | flops 1073741824 | bytes 4194304 | tf_op jit(solution)/shard_map/project_out/pallas_call | solution.py:209
  116.3 4.2 %all-to-all-done.3.d_parts = bf16[4,256,1024]{2,1,0:T(8,128)(2,1)S(1)} async-done(((bf16[4,256,1024]{2,1,0:T(8,128)(2,1)}), bf16[4,256,1024]{2,1,0:T(8,128)(2,1)S(1)}, u32[]{:S(2)}, u32[]{:S(2)}) %all-to-all-start.3) | async-done | bytes 2097184 | tf_op jit(solution)/shard_map/all_to_all | solution.py:226
  120.4 8.5 %all-to-all-start.4 = ((bf16[16,256,128]{2,1,0:T(8,128)(2,1)}), bf16[16,256,128]{2,1,0:T(8,128)(2,1)S(1)}, u32[]{:S(2)}, u32[]{:S(2)}) async-start(bf16[16,256,128]{2,1,0:T(8,128)(2,1)} %bitcast.28), calls=%async_computation.4 | async-start | bytes 2097152 | tf_op jit(solution)/shard_map/all_to_all | solution.py:226
  128.9 7.2 %shard_map.95 = (bf16[256,1024]{1,0:T(8,128)(2,1)}, bf16[512,128]{1,0:T(8,128)(2,1)}, bf16[512,128]{1,0:T(8,128)(2,1)}, f32[512,128]{1,0:T(8,128)}) custom-call(bf16[256,1024]{1,0:T(8,128)(2,1)} %q.3, bf16[512,128]{1,0:T(8,128)(2,1)} %copy-done.7, bf16[512,128]{1,0:T(8,128)(2,1)} %copy-done.8, bf16[512,128]{1,0:T(8,128)(2,1)} %copy-done.6, ...), custom_call_target="tpu_custom_call" | custom-call | flops 8589934592 | bytes 8388608 | tf_op jit(solution)/shard_map/pallas_call | solution.py:144
  136.1 7.5 %collective-permute-start.7 = (bf16[512,128]{1,0:T(8,128)(2,1)}, bf16[512,128]{1,0:T(8,128)(2,1)S(1)}, u32[]{:S(2)}, u32[]{:S(2)}) collective-permute-start(bf16[512,128]{1,0:T(8,128)(2,1)} %get-tuple-element.19), channel_id=1, source_target_pairs={{8,0},{16,8},{24,16},{32,24},{40,32},{48,40},{56,48},{64,56},{72,6... | collective-permute-start | bytes 393224 | tf_op jit(solution)/shard_map/ppermute | solution.py:235
  143.6 2.8 %collective-permute-start.6 = (bf16[512,128]{1,0:T(8,128)(2,1)}, bf16[512,128]{1,0:T(8,128)(2,1)S(1)}, u32[]{:S(2)}, u32[]{:S(2)}) collective-permute-start(bf16[512,128]{1,0:T(8,128)(2,1)} %get-tuple-element.18), channel_id=1, source_target_pairs={{16,0},{24,8},{32,16},{40,24},{48,32},{56,40},{64,48},{72,56},{80,... | collective-permute-start | bytes 393224 | tf_op jit(solution)/shard_map/ppermute | solution.py:235
  147.4 4.8 %collective-permute-done.6 = bf16[512,128]{1,0:T(8,128)(2,1)S(1)} collective-permute-done((bf16[512,128]{1,0:T(8,128)(2,1)}, bf16[512,128]{1,0:T(8,128)(2,1)S(1)}, u32[]{:S(2)}, u32[]{:S(2)}) %collective-permute-start.6) | collective-permute-done | bytes 131104 | tf_op jit(solution)/shard_map/ppermute | solution.py:235
  (40 shorter events, 10.1 us)
Async XLA Ops:
  7.2 13.1 %copy-start.2 = (bf16[256,512]{1,0:T(8,128)(2,1)S(1)}, bf16[256,512]{1,0:T(8,128)(2,1)}, u32[]{:S(2)}) copy-start(bf16[256,512]{1,0:T(8,128)(2,1)} %param.9) | copy-start | bytes 786436
  7.2 73.0 %all-gather.2.cloned.1.call-start = ((), (), s32[]{:S(2)}) async-start(), calls=%async_computation.5 | async-start | bytes 2359296 | tf_op jit(solution)/shard_map/all_gather | solution.py:259
  31.2 4.6 %copy-start.4 = (bf16[256,128]{1,0:T(8,128)(2,1)S(1)}, bf16[256,128]{1,0:T(8,128)(2,1)}, u32[]{:S(2)}) copy-start(bf16[256,128]{1,0:T(8,128)(2,1)} %param.7) | copy-start | bytes 196612
  31.3 4.6 %copy-start.5 = (bf16[256,128]{1,0:T(8,128)(2,1)S(1)}, bf16[256,128]{1,0:T(8,128)(2,1)}, u32[]{:S(2)}) copy-start(bf16[256,128]{1,0:T(8,128)(2,1)} %param.8) | copy-start | bytes 196612
  31.3 47.2 %all-to-all-start.1 = ((bf16[8,1024,128]{2,1,0:T(8,128)(2,1)}), bf16[8,1024,128]{2,1,0:T(8,128)(2,1)S(1)}, u32[]{:S(2)}, u32[]{:S(2)}) async-start(bf16[8,1024,128]{2,1,0:T(8,128)(2,1)} %broadcast_in_dim.8), calls=%async_computation.1 | async-start | bytes 4194304 | tf_op jit(solution)/shard_map/all_to_all | solution.py:226
  35.9 25.1 %copy-start.6 = (bf16[512,128]{1,0:T(8,128)(2,1)}, bf16[512,128]{1,0:T(8,128)(2,1)S(1)}, u32[]{:S(2)}) copy-start(bf16[512,128]{1,0:T(8,128)(2,1)S(1)} %constant_dynamic-update-slice_fusion.k0.v0) | copy-start | bytes 393220
  35.9 17.0 %collective-permute-start = (bf16[512,128]{1,0:T(8,128)(2,1)S(1)}, bf16[512,128]{1,0:T(8,128)(2,1)S(1)}, u32[]{:S(2)}, u32[]{:S(2)}) collective-permute-start(bf16[512,128]{1,0:T(8,128)(2,1)S(1)} %constant_dynamic-update-slice_fusion.k0.v0), channel_id=1, source_target_pairs={{0,16},{8,24},{16,32},{24,40},{32,48},{40,56},{48,64},{56,72},{64,... | collective-permute-start | bytes 393224 | tf_op jit(solution)/shard_map/ppermute | solution.py:235
  38.7 22.4 %collective-permute-start.1 = (bf16[512,128]{1,0:T(8,128)(2,1)S(1)}, bf16[512,128]{1,0:T(8,128)(2,1)S(1)}, u32[]{:S(2)}, u32[]{:S(2)}) collective-permute-start(bf16[512,128]{1,0:T(8,128)(2,1)S(1)} %constant_dynamic-update-slice_fusion.k0.v0), channel_id=1, source_target_pairs={{0,8},{8,16},{16,24},{24,32},{32,40},{40,48},{48,56},{56,64},{64,7... | collective-permute-start | bytes 393224 | tf_op jit(solution)/shard_map/ppermute | solution.py:235
  52.9 8.1 %copy-start.7 = (bf16[512,128]{1,0:T(8,128)(2,1)}, bf16[512,128]{1,0:T(8,128)(2,1)S(1)}, u32[]{:S(2)}) copy-start(bf16[512,128]{1,0:T(8,128)(2,1)S(1)} %collective-permute-done.k2.v2) | copy-start | bytes 393220
  61.0 0.7 copy-start.8
  69.5 28.3 %collective-permute-start.2 = (bf16[256,1024]{1,0:T(8,128)(2,1)}, bf16[256,1024]{1,0:T(8,128)(2,1)}, u32[]{:S(2)}, u32[]{:S(2)}) collective-permute-start(bf16[256,1024]{1,0:T(8,128)(2,1)} %get-tuple-element.12.att.refs_0_), channel_id=1, source_target_pairs={{0,8},{8,16},{16,24},{24,0},{1,9},{9,17},{17,25},{25,1},{2,10},{10... | collective-permute-start | bytes 1572872 | tf_op jit(solution)/shard_map/ppermute | solution.py:245
  71.4 26.3 %collective-permute-start.3 = (bf16[256,1024]{1,0:T(8,128)(2,1)}, bf16[256,1024]{1,0:T(8,128)(2,1)}, u32[]{:S(2)}, u32[]{:S(2)}) collective-permute-start(bf16[256,1024]{1,0:T(8,128)(2,1)} %get-tuple-element.12.att.refs_0_), channel_id=1, source_target_pairs={{0,16},{8,24},{16,0},{24,8},{1,17},{9,25},{17,1},{25,9},{2,18},{10... | collective-permute-start | bytes 1572872 | tf_op jit(solution)/shard_map/ppermute | solution.py:245
  73.3 28.4 %collective-permute-start.4 = (bf16[256,1024]{1,0:T(8,128)(2,1)}, bf16[256,1024]{1,0:T(8,128)(2,1)}, u32[]{:S(2)}, u32[]{:S(2)}) collective-permute-start(bf16[256,1024]{1,0:T(8,128)(2,1)} %get-tuple-element.12.att.refs_0_), channel_id=1, source_target_pairs={{0,24},{8,0},{16,8},{24,16},{1,25},{9,1},{17,9},{25,17},{2,26},{10... | collective-permute-start | bytes 1572872 | tf_op jit(solution)/shard_map/ppermute | solution.py:245
  86.4 34.1 %all-to-all-start.3 = ((bf16[4,256,1024]{2,1,0:T(8,128)(2,1)}), bf16[4,256,1024]{2,1,0:T(8,128)(2,1)S(1)}, u32[]{:S(2)}, u32[]{:S(2)}) async-start(bf16[4,256,1024]{2,1,0:T(8,128)(2,1)} %shard_map.93.refs_6_), calls=%async_computation.3 | async-start | bytes 4194304 | tf_op jit(solution)/shard_map/all_to_all | solution.py:226
  105.9 4.8 %collective-permute-start.5 = (bf16[4,1024,128]{2,1,0:T(8,128)(2,1)}, bf16[4,1024,128]{2,1,0:T(8,128)(2,1)S(1)}, u32[]{:S(2)}, u32[]{:S(2)}) collective-permute-start(bf16[4,1024,128]{2,1,0:T(8,128)(2,1)} %project_out.2), channel_id=1, source_target_pairs={{0,1},{1,0},{2,3},{3,2},{4,5},{5,4},{6,7},{7,6},{8,9},{9,8},{10,11... | collective-permute-start | bytes 3145736 | tf_op jit(solution)/shard_map/ppermute | solution.py:239
  110.7 1.1 copy-start.1
  120.4 8.5 %copy-start = (bf16[4,256,1024]{2,1,0:T(8,128)(2,1)}, bf16[4,256,1024]{2,1,0:T(8,128)(2,1)S(1)}, u32[]{:S(2)}) copy-start(bf16[4,256,1024]{2,1,0:T(8,128)(2,1)S(1)} %all-to-all-done.3.d_parts) | copy-start | bytes 6291460
  120.4 25.9 %all-to-all-start.4 = ((bf16[16,256,128]{2,1,0:T(8,128)(2,1)}), bf16[16,256,128]{2,1,0:T(8,128)(2,1)S(1)}, u32[]{:S(2)}, u32[]{:S(2)}) async-start(bf16[16,256,128]{2,1,0:T(8,128)(2,1)} %bitcast.28), calls=%async_computation.4 | async-start | bytes 2097152 | tf_op jit(solution)/shard_map/all_to_all | solution.py:226
  136.1 16.1 %copy-start.3 = (f32[512,128]{1,0:T(8,128)S(1)}, f32[512,128]{1,0:T(8,128)}, u32[]{:S(2)}) copy-start(f32[512,128]{1,0:T(8,128)} %get-tuple-element.17) | copy-start | bytes 786436
  136.1 11.2 %collective-permute-start.7 = (bf16[512,128]{1,0:T(8,128)(2,1)}, bf16[512,128]{1,0:T(8,128)(2,1)S(1)}, u32[]{:S(2)}, u32[]{:S(2)}) collective-permute-start(bf16[512,128]{1,0:T(8,128)(2,1)} %get-tuple-element.19), channel_id=1, source_target_pairs={{8,0},{16,8},{24,16},{32,24},{40,32},{48,40},{56,48},{64,56},{72,6... | collective-permute-start | bytes 393224 | tf_op jit(solution)/shard_map/ppermute | solution.py:235
  143.6 8.6 %collective-permute-start.6 = (bf16[512,128]{1,0:T(8,128)(2,1)}, bf16[512,128]{1,0:T(8,128)(2,1)S(1)}, u32[]{:S(2)}, u32[]{:S(2)}) collective-permute-start(bf16[512,128]{1,0:T(8,128)(2,1)} %get-tuple-element.18), channel_id=1, source_target_pairs={{16,0},{24,8},{32,16},{40,24},{48,32},{56,40},{64,48},{72,56},{80,... | collective-permute-start | bytes 393224 | tf_op jit(solution)/shard_map/ppermute | solution.py:235
Sparse Core Ops, SparseCore 0:
  20.4 59.2 all-gather.1

commit v4 on v3

--- a/solution.py
+++ b/solution.py
@@ -13,7 +13,7 @@
 LOG2E = 1.4426950408889634
 NT = (((1,), (1,)), ((), ()))
 HEAD = ("y", "core")
-DP = ("z_far", "z_pair", "x")
+DP = ("z_pair", "z_far", "x")
 BF = jnp.bfloat16
 F32 = jnp.float32
 HEADS = 8
@@ -162,20 +162,22 @@
 
 def back_body(cot, w, out):
     rows = out.shape[1]
-    done = dot_nt(cot[...], w[...]).astype(BF)
+    done = dot_nt(cot[...], w[:, 0].reshape(-1, w.shape[-1])).astype(BF)
     for b in range(out.shape[0]):
         out[b] = done[b * rows : (b + 1) * rows]
 
 
 def project_back(cot, w, parts, block=256):
     tokens, columns = cot.shape
-    inner = w.shape[0]
+    far, pair, deep, _ = w.shape
+    inner = far * pair * deep
     rows = tokens // parts
+    count = block // deep
     return call(
         back_body,
         2 << 30,
         grid=(inner // block,),
-        in_specs=[pl.BlockSpec((tokens, columns), lambda i: (0, 0)), pl.BlockSpec((block, columns), lambda i: (i, 0))],
+        in_specs=[pl.BlockSpec((tokens, columns), lambda i: (0, 0)), pl.BlockSpec((count, 1, deep, columns), lambda i: (lax.rem(i, far // count), lax.div(i, far // count), 0, 0))],
         out_specs=pl.BlockSpec((parts, rows, block), lambda i: (0, 0, i)),
         out_shape=jax.ShapeDtypeStruct((parts, rows, inner), BF),
     )(cot, w)
@@ -192,7 +194,8 @@
             owner = lax.rem(index[0] + parts - k, parts)
             lhs[pl.ds(pl.multiple_of(owner * rows, rows), rows), :] = block[...]
 
-    done = dot_nn(lhs[...], jnp.concatenate([w0[...], w1[...]], axis=1))
+    by_z = [jnp.concatenate([w[:, b].reshape(-1, HD) for b in range(w.shape[1])], axis=0) for w in (w0, w1)]
+    done = dot_nn(lhs[...], jnp.concatenate(by_z, axis=1))
     for n in range(2):
         value = done[:, n * HD : (n + 1) * HD]
         for more in add:
@@ -205,7 +208,7 @@
     parts = len(blocks)
     whole = pl.BlockSpec(memory_space=pltpu.VMEM)
     part = pl.BlockSpec((2, parts * rows, HD), lambda i, x, s: (i, 0, 0))
-    columns = [pl.BlockSpec((inner, HD), lambda i, x, s, n=n: (0, 4 * i + 2 * n + s[0])) for n in range(2)]
+    columns = [pl.BlockSpec((*w.shape[:3], HD), lambda i, x, s, n=n: (0, 0, 0, 4 * i + 2 * n + s[0])) for n in range(2)]
     return pl.pallas_call(
         functools.partial(out_body, parts),
         grid_spec=pltpu.PrefetchScalarGridSpec(
@@ -256,7 +259,7 @@
     own_w = out_weight.reshape(few, HEADS, parts, HD).transpose(2, 0, 1, 3).reshape(parts, few, HEADS * HD)
     own_w = jnp.concatenate([own_w] * 2, axis=0)
     own_w = swap(own_w, ("z_pair", "x")).reshape(-1, HEADS * HD)
-    weight = lax.all_gather(own_w, "z_far", axis=0, tiled=True)
+    weight = lax.all_gather(own_w, "z_far", axis=0, tiled=True).reshape(-1, 2, parts * few, HEADS * HD)
     pair = jnp.concatenate([keys, values], axis=0)
     pairs = [shifted(pair, 2), shifted(pair, 1), pair]
     own_g = output_grad.reshape(rows, parts, HD).transpose(1, 0, 2)
@@ -283,7 +286,7 @@
 
 
 def solution(mesh):
-    finer = Mesh(mesh.devices.reshape(8, 2, 4, 4, 2), ("z_far", "z_pair", "x", "y", "core"))
+    finer = Mesh(mesh.devices.reshape(2, 8, 4, 4, 2), ("z_pair", "z_far", "x", "y", "core"))
     token = P(DP, HEAD)
 
     return jax.shard_map(

time: 160 us -> 183 us (1.14)
  the two profiles are of different devices: /device:TPU:384 before, /device:TPU:32 now
where the time goes in v4:
time: 183 us; the launch traced here: 182 us
  blocking collectives  50 us (27%)
  starting transfers between devices  46.8 us (26%)
  waiting for transfers between devices  32.9 us (18%)
  Pallas kernels  29.8 us (16%)
  between operations  14.3 us (8%)
  local copies, waits for them, and re-layouts  6.5 us (4%)
    all_to_all x2, blocking collectives, swap(): return lax.all_to_all(pieces, axis, 0, 0, tiled=True)  50 us
    all_to_all x3, starting transfers between devices, swap(): return lax.all_to_all(pieces, axis, 0, 0, tiled=True)  19.4 us
    ppermute x4, waiting for transfers between devices, shifted(): lax.ppermute(block, DP, [(i, i + distance) for i in range(size) if 0 <= i...  17.3 us
    ppermute x4, starting transfers between devices, shifted(): lax.ppermute(block, DP, [(i, i + distance) for i in range(size) if 0 <= i...  16.5 us
    ppermute x3, starting transfers between devices, around(): lax.ppermute(blocks[k], axis, [(i, (i + k * step) % size) for i in range(...  8.97 us
    pallas_call x2, Pallas kernels, project_out(): pl.pallas_call(functools.partial(out_body, parts), grid_spec=pltpu.Prefet...  8.72 us
    pallas_call x1, Pallas kernels, forward(): call(functools.partial(forward_body, 1.0 / math.sqrt(HD), group), 8 << 30...  7.77 us
    all_to_all x3, waiting for transfers between devices, swap(): return lax.all_to_all(pieces, axis, 0, 0, tiled=True)  7.31 us
  transfers between devices with their start and end apart: 12, of which 6 were waited for; matrix products, arithmetic and copies ran while one was open for 3% of the time, Pallas kernels for 16%

profile of v4, /device:TPU:32, one launch (start us, length us, event | category | flops | bytes accessed | tf_op | source)
XLA Modules:
  0.0 181.9 jit_solution(1988729299409833325)
XLA Ops:
  8.4 40.9 %all_to_all.25 = bf16[8,16,1024]{2,1,0:T(8,128)(2,1)} all-to-all(bf16[8,16,1024]{2,1,0:T(8,128)(2,1)S(1)} %pad_maximum_fusion), channel_id=1, replica_groups=mesh['z_pair'=2,'z_far'=8,'x'=4,'y'=4,'core'=2] {'z_pair','x'}, dimensions={0} | all-to-all | bytes 524288 | tf_op jit(solution)/shard_map/all_to_all | solution.py:229
  49.4 9.1 %all_to_all.26 = bf16[4,256,128]{1,2,0:T(8,128)(2,1)S(1)} all-to-all(bf16[4,256,128]{1,2,0:T(8,128)(2,1)S(1)} %bitcast.39), channel_id=1, replica_groups=mesh['z_pair'=2,'z_far'=8,'x'=4,'y'=4,'core'=2] {'x'}, dimensions={0} | all-to-all | bytes 524288 | tf_op jit(solution)/shard_map/all_to_all | solution.py:229
  60.3 4.6 %all-to-all-start.1 = ((bf16[8,1024,128]{2,1,0:T(8,128)(2,1)}), bf16[8,1024,128]{2,1,0:T(8,128)(2,1)S(1)}, u32[]{:S(2)}, u32[]{:S(2)}) async-start(bf16[8,1024,128]{2,1,0:T(8,128)(2,1)} %broadcast_in_dim.8), calls=%async_computation.1 | async-start | bytes 4194304 | tf_op jit(solution)/shard_map/all_to_all | solution.py:229
  64.9 2.7 %collective-permute-start = (bf16[512,128]{1,0:T(8,128)(2,1)S(1)}, bf16[512,128]{1,0:T(8,128)(2,1)S(1)}, u32[]{:S(2)}, u32[]{:S(2)}) collective-permute-start(bf16[512,128]{1,0:T(8,128)(2,1)S(1)} %constant_dynamic-update-slice_fusion.k0.v0), channel_id=1, source_target_pairs={{0,16},{8,24},{16,32},{24,40},{32,48},{40,56},{48,64},{56,72},{64,... | collective-permute-start | bytes 393224 | tf_op jit(solution)/shard_map/ppermute | solution.py:238
  67.7 3.1 %collective-permute-start.1 = (bf16[512,128]{1,0:T(8,128)(2,1)S(1)}, bf16[512,128]{1,0:T(8,128)(2,1)S(1)}, u32[]{:S(2)}, u32[]{:S(2)}) collective-permute-start(bf16[512,128]{1,0:T(8,128)(2,1)S(1)} %constant_dynamic-update-slice_fusion.k0.v0), channel_id=1, source_target_pairs={{0,8},{8,16},{16,24},{24,32},{32,40},{40,48},{48,56},{56,64},{64,7... | collective-permute-start | bytes 393224 | tf_op jit(solution)/shard_map/ppermute | solution.py:238
  70.8 7.1 %collective-permute-done.k2.v2 = bf16[512,128]{1,0:T(8,128)(2,1)S(1)} collective-permute-done((bf16[512,128]{1,0:T(8,128)(2,1)S(1)}, bf16[512,128]{1,0:T(8,128)(2,1)S(1)}, u32[]{:S(2)}, u32[]{:S(2)}) %collective-permute-start) | collective-permute-done | bytes 131104 | tf_op jit(solution)/shard_map/ppermute | solution.py:238
  77.9 5.3 %collective-permute-done.1.k1.v1 = bf16[512,128]{1,0:T(8,128)(2,1)S(1)} collective-permute-done((bf16[512,128]{1,0:T(8,128)(2,1)S(1)}, bf16[512,128]{1,0:T(8,128)(2,1)S(1)}, u32[]{:S(2)}, u32[]{:S(2)}) %collective-permute-start.1) | collective-permute-done | bytes 131104 | tf_op jit(solution)/shard_map/ppermute | solution.py:238
  83.9 7.8 %shard_map.94 = (bf16[256,1024]{1,0:T(8,128)(2,1)}, bf16[8,768,256]{2,1,0:T(8,128)(2,1)}) custom-call(s32[64]{0:T(128)} %lengths.1, s32[1]{0:T(128)} %bitcast.7.place, bf16[256,1024]{1,0:T(8,128)(2,1)} %q.3, bf16[512,128]{1,0:T(8,128)(2,1)} %copy-done.7, bf16[512,128]{1,0:T(8,128)(2,1)} %copy-done.8, bf16[512,128]{1,0:T(8,128)(2,1)} %copy-done.6, ...), custom_call_target="tpu_custom_call" | custom-call | flops 8589934592 | bytes 8388608 | tf_op jit(solution)/shard_map/pallas_call | solution.py:86
  91.7 1.9 %collective-permute-start.2 = (bf16[256,1024]{1,0:T(8,128)(2,1)}, bf16[256,1024]{1,0:T(8,128)(2,1)}, u32[]{:S(2)}, u32[]{:S(2)}) collective-permute-start(bf16[256,1024]{1,0:T(8,128)(2,1)} %get-tuple-element.12.att.refs_0_), channel_id=1, source_target_pairs={{0,8},{8,16},{16,24},{24,0},{1,9},{9,17},{17,25},{25,1},{2,10},{10... | collective-permute-start | bytes 1572872 | tf_op jit(solution)/shard_map/ppermute | solution.py:248
  93.6 1.9 %collective-permute-start.3 = (bf16[256,1024]{1,0:T(8,128)(2,1)}, bf16[256,1024]{1,0:T(8,128)(2,1)}, u32[]{:S(2)}, u32[]{:S(2)}) collective-permute-start(bf16[256,1024]{1,0:T(8,128)(2,1)} %get-tuple-element.12.att.refs_0_), channel_id=1, source_target_pairs={{0,16},{8,24},{16,0},{24,8},{1,17},{9,25},{17,1},{25,9},{2,18},{10... | collective-permute-start | bytes 1572872 | tf_op jit(solution)/shard_map/ppermute | solution.py:248
  95.5 5.1 %collective-permute-start.4 = (bf16[256,1024]{1,0:T(8,128)(2,1)}, bf16[256,1024]{1,0:T(8,128)(2,1)}, u32[]{:S(2)}, u32[]{:S(2)}) collective-permute-start(bf16[256,1024]{1,0:T(8,128)(2,1)} %get-tuple-element.12.att.refs_0_), channel_id=1, source_target_pairs={{0,24},{8,0},{16,8},{24,16},{1,25},{9,1},{17,9},{25,17},{2,26},{10... | collective-permute-start | bytes 1572872 | tf_op jit(solution)/shard_map/ppermute | solution.py:248
  102.4 5.5 %all-gather.2.cloned.1.call-done = bf16[1024,1024]{1,0:T(8,128)(2,1)} async-done(((bf16[128,1024]{1,0:T(8,128)(2,1)}), bf16[1024,1024]{1,0:T(8,128)(2,1)}) %all-gather.2.cloned.1.call-update) | async-done | bytes 2097168 | tf_op jit(solution)/shard_map/all_gather | solution.py:262
  107.9 6.2 %shard_map.93.refs_6_ = bf16[4,256,1024]{2,1,0:T(8,128)(2,1)} custom-call(bf16[1024,1024]{1,0:T(8,128)(2,1)} %copy_bitcast_fusion.cot, bf16[8,2,64,1024]{3,2,1,0:T(8,128)(2,1)} %bitcast.30), custom_call_target="tpu_custom_call" | custom-call | flops 2147483648 | bytes 8388608 | tf_op jit(solution)/shard_map/pallas_call | solution.py:176
  114.1 9.0 %all-to-all-start.3 = ((bf16[4,256,1024]{2,1,0:T(8,128)(2,1)}), bf16[4,256,1024]{2,1,0:T(8,128)(2,1)S(1)}, u32[]{:S(2)}, u32[]{:S(2)}) async-start(bf16[4,256,1024]{2,1,0:T(8,128)(2,1)} %shard_map.93.refs_6_), calls=%async_computation.3 | async-start | bytes 4194304 | tf_op jit(solution)/shard_map/all_to_all | solution.py:229
  123.0 4.2 %project_out.2 = bf16[4,1024,128]{2,1,0:T(8,128)(2,1)} custom-call(s32[1]{0:T(128)} %bitcast.8.index, s32[1]{0:T(128)S(6)} %sub.3.side, bf16[256,1024]{1,0:T(8,128)(2,1)} %get-tuple-element.12.att.refs_0_, bf16[256,1024]{1,0:T(8,128)(2,1)} %collective-permute-done.2.refs_1_, bf16[256,1024]{1,0:T(8,128)(2,1)} %collective-permute-done.3.refs_2_, ...), custom_call_target="tpu_custom_call" | custom-call | flops 1073741824 | bytes 4194304 | tf_op jit(solution)/shard_map/project_out/pallas_call | solution.py:212
  127.2 1.9 %collective-permute-start.5 = (bf16[4,1024,128]{2,1,0:T(8,128)(2,1)}, bf16[4,1024,128]{2,1,0:T(8,128)(2,1)S(1)}, u32[]{:S(2)}, u32[]{:S(2)}) collective-permute-start(bf16[4,1024,128]{2,1,0:T(8,128)(2,1)} %project_out.2), channel_id=1, source_target_pairs={{0,1},{1,0},{2,3},{3,2},{4,5},{5,4},{6,7},{7,6},{8,9},{9,8},{10,11... | collective-permute-start | bytes 3145736 | tf_op jit(solution)/shard_map/ppermute | solution.py:242
  129.1 2.8 %collective-permute-done.5.refs_7_ = bf16[4,1024,128]{2,1,0:T(8,128)(2,1)S(1)} collective-permute-done((bf16[4,1024,128]{2,1,0:T(8,128)(2,1)}, bf16[4,1024,128]{2,1,0:T(8,128)(2,1)S(1)}, u32[]{:S(2)}, u32[]{:S(2)}) %collective-permute-start.5) | collective-permute-done | bytes 1048608 | tf_op jit(solution)/shard_map/ppermute | solution.py:242
  133.1 4.5 %project_out.3 = bf16[4,1024,128]{2,1,0:T(8,128)(2,1)} custom-call(s32[1]{0:T(128)} %bitcast.8.index, s32[1]{0:T(128)} %bitcast.9.side, bf16[256,1024]{1,0:T(8,128)(2,1)} %get-tuple-element.12.att.refs_0_, bf16[256,1024]{1,0:T(8,128)(2,1)} %collective-permute-done.2.refs_1_, bf16[256,1024]{1,0:T(8,128)(2,1)} %collective-permute-done.3.refs_2_, ...), custom_call_target="tpu_custom_call" | custom-call | flops 1073741824 | bytes 4194304 | tf_op jit(solution)/shard_map/project_out/pallas_call | solution.py:212
  137.6 7.3 %all-to-all-done.3.d_parts = bf16[4,256,1024]{2,1,0:T(8,128)(2,1)S(1)} async-done(((bf16[4,256,1024]{2,1,0:T(8,128)(2,1)}), bf16[4,256,1024]{2,1,0:T(8,128)(2,1)S(1)}, u32[]{:S(2)}, u32[]{:S(2)}) %all-to-all-start.3) | async-done | bytes 2097184 | tf_op jit(solution)/shard_map/all_to_all | solution.py:229
  144.9 5.8 %all-to-all-start.4 = ((bf16[16,256,128]{2,1,0:T(8,128)(2,1)}), bf16[16,256,128]{2,1,0:T(8,128)(2,1)S(1)}, u32[]{:S(2)}, u32[]{:S(2)}) async-start(bf16[16,256,128]{2,1,0:T(8,128)(2,1)} %bitcast.36), calls=%async_computation.4 | async-start | bytes 2097152 | tf_op jit(solution)/shard_map/all_to_all | solution.py:229
  150.7 7.2 %shard_map.95 = (bf16[256,1024]{1,0:T(8,128)(2,1)}, bf16[512,128]{1,0:T(8,128)(2,1)}, bf16[512,128]{1,0:T(8,128)(2,1)}, f32[512,128]{1,0:T(8,128)}) custom-call(bf16[256,1024]{1,0:T(8,128)(2,1)} %q.3, bf16[512,128]{1,0:T(8,128)(2,1)} %copy-done.7, bf16[512,128]{1,0:T(8,128)(2,1)} %copy-done.8, bf16[512,128]{1,0:T(8,128)(2,1)} %copy-done.6, ...), custom_call_target="tpu_custom_call" | custom-call | flops 8589934592 | bytes 8388608 | tf_op jit(solution)/shard_map/pallas_call | solution.py:144
  157.9 7.9 %collective-permute-start.7 = (bf16[512,128]{1,0:T(8,128)(2,1)}, bf16[512,128]{1,0:T(8,128)(2,1)S(1)}, u32[]{:S(2)}, u32[]{:S(2)}) collective-permute-start(bf16[512,128]{1,0:T(8,128)(2,1)} %get-tuple-element.19), channel_id=1, source_target_pairs={{8,0},{16,8},{24,16},{32,24},{40,32},{48,40},{56,48},{64,56},{72,6... | collective-permute-start | bytes 393224 | tf_op jit(solution)/shard_map/ppermute | solution.py:238
  165.8 2.8 %collective-permute-start.6 = (bf16[512,128]{1,0:T(8,128)(2,1)}, bf16[512,128]{1,0:T(8,128)(2,1)S(1)}, u32[]{:S(2)}, u32[]{:S(2)}) collective-permute-start(bf16[512,128]{1,0:T(8,128)(2,1)} %get-tuple-element.18), channel_id=1, source_target_pairs={{16,0},{24,8},{32,16},{40,24},{48,32},{56,40},{64,48},{72,56},{80,... | collective-permute-start | bytes 393224 | tf_op jit(solution)/shard_map/ppermute | solution.py:238
  169.6 4.8 %collective-permute-done.6 = bf16[512,128]{1,0:T(8,128)(2,1)S(1)} collective-permute-done((bf16[512,128]{1,0:T(8,128)(2,1)}, bf16[512,128]{1,0:T(8,128)(2,1)S(1)}, u32[]{:S(2)}, u32[]{:S(2)}) %collective-permute-start.6) | collective-permute-done | bytes 131104 | tf_op jit(solution)/shard_map/ppermute | solution.py:238
  (40 shorter events, 8.2 us)
Async XLA Ops:
  7.2 42.1 %copy-start.2 = (bf16[256,512]{1,0:T(8,128)(2,1)S(1)}, bf16[256,512]{1,0:T(8,128)(2,1)}, u32[]{:S(2)}) copy-start(bf16[256,512]{1,0:T(8,128)(2,1)} %param.9) | copy-start | bytes 786436
  7.2 100.7 %all-gather.2.cloned.1.call-start = ((), (), s32[]{:S(2)}) async-start(), calls=%async_computation.5 | async-start | bytes 2359296 | tf_op jit(solution)/shard_map/all_gather | solution.py:262
  60.3 4.6 %copy-start.4 = (bf16[256,128]{1,0:T(8,128)(2,1)S(1)}, bf16[256,128]{1,0:T(8,128)(2,1)}, u32[]{:S(2)}) copy-start(bf16[256,128]{1,0:T(8,128)(2,1)} %param.7) | copy-start | bytes 196612
  60.3 4.6 %copy-start.5 = (bf16[256,128]{1,0:T(8,128)(2,1)S(1)}, bf16[256,128]{1,0:T(8,128)(2,1)}, u32[]{:S(2)}) copy-start(bf16[256,128]{1,0:T(8,128)(2,1)} %param.8) | copy-start | bytes 196612
  60.3 40.4 %all-to-all-start.1 = ((bf16[8,1024,128]{2,1,0:T(8,128)(2,1)}), bf16[8,1024,128]{2,1,0:T(8,128)(2,1)S(1)}, u32[]{:S(2)}, u32[]{:S(2)}) async-start(bf16[8,1024,128]{2,1,0:T(8,128)(2,1)} %broadcast_in_dim.8), calls=%async_computation.1 | async-start | bytes 4194304 | tf_op jit(solution)/shard_map/all_to_all | solution.py:229
  64.9 18.3 %copy-start.6 = (bf16[512,128]{1,0:T(8,128)(2,1)}, bf16[512,128]{1,0:T(8,128)(2,1)S(1)}, u32[]{:S(2)}) copy-start(bf16[512,128]{1,0:T(8,128)(2,1)S(1)} %constant_dynamic-update-slice_fusion.k0.v0) | copy-start | bytes 393220
  64.9 13.0 %collective-permute-start = (bf16[512,128]{1,0:T(8,128)(2,1)S(1)}, bf16[512,128]{1,0:T(8,128)(2,1)S(1)}, u32[]{:S(2)}, u32[]{:S(2)}) collective-permute-start(bf16[512,128]{1,0:T(8,128)(2,1)S(1)} %constant_dynamic-update-slice_fusion.k0.v0), channel_id=1, source_target_pairs={{0,16},{8,24},{16,32},{24,40},{32,48},{40,56},{48,64},{56,72},{64,... | collective-permute-start | bytes 393224 | tf_op jit(solution)/shard_map/ppermute | solution.py:238
  67.7 15.6 %collective-permute-start.1 = (bf16[512,128]{1,0:T(8,128)(2,1)S(1)}, bf16[512,128]{1,0:T(8,128)(2,1)S(1)}, u32[]{:S(2)}, u32[]{:S(2)}) collective-permute-start(bf16[512,128]{1,0:T(8,128)(2,1)S(1)} %constant_dynamic-update-slice_fusion.k0.v0), channel_id=1, source_target_pairs={{0,8},{8,16},{16,24},{24,32},{32,40},{40,48},{48,56},{56,64},{64,7... | collective-permute-start | bytes 393224 | tf_op jit(solution)/shard_map/ppermute | solution.py:238
  77.9 5.3 %copy-start.7 = (bf16[512,128]{1,0:T(8,128)(2,1)}, bf16[512,128]{1,0:T(8,128)(2,1)S(1)}, u32[]{:S(2)}) copy-start(bf16[512,128]{1,0:T(8,128)(2,1)S(1)} %collective-permute-done.k2.v2) | copy-start | bytes 393220
  83.3 0.7 copy-start.8
  91.7 31.3 %collective-permute-start.2 = (bf16[256,1024]{1,0:T(8,128)(2,1)}, bf16[256,1024]{1,0:T(8,128)(2,1)}, u32[]{:S(2)}, u32[]{:S(2)}) collective-permute-start(bf16[256,1024]{1,0:T(8,128)(2,1)} %get-tuple-element.12.att.refs_0_), channel_id=1, source_target_pairs={{0,8},{8,16},{16,24},{24,0},{1,9},{9,17},{17,25},{25,1},{2,10},{10... | collective-permute-start | bytes 1572872 | tf_op jit(solution)/shard_map/ppermute | solution.py:248
  93.6 29.4 %collective-permute-start.3 = (bf16[256,1024]{1,0:T(8,128)(2,1)}, bf16[256,1024]{1,0:T(8,128)(2,1)}, u32[]{:S(2)}, u32[]{:S(2)}) collective-permute-start(bf16[256,1024]{1,0:T(8,128)(2,1)} %get-tuple-element.12.att.refs_0_), channel_id=1, source_target_pairs={{0,16},{8,24},{16,0},{24,8},{1,17},{9,25},{17,1},{25,9},{2,18},{10... | collective-permute-start | bytes 1572872 | tf_op jit(solution)/shard_map/ppermute | solution.py:248
  95.5 27.5 %collective-permute-start.4 = (bf16[256,1024]{1,0:T(8,128)(2,1)}, bf16[256,1024]{1,0:T(8,128)(2,1)}, u32[]{:S(2)}, u32[]{:S(2)}) collective-permute-start(bf16[256,1024]{1,0:T(8,128)(2,1)} %get-tuple-element.12.att.refs_0_), channel_id=1, source_target_pairs={{0,24},{8,0},{16,8},{24,16},{1,25},{9,1},{17,9},{25,17},{2,26},{10... | collective-permute-start | bytes 1572872 | tf_op jit(solution)/shard_map/ppermute | solution.py:248
  114.1 30.8 %all-to-all-start.3 = ((bf16[4,256,1024]{2,1,0:T(8,128)(2,1)}), bf16[4,256,1024]{2,1,0:T(8,128)(2,1)S(1)}, u32[]{:S(2)}, u32[]{:S(2)}) async-start(bf16[4,256,1024]{2,1,0:T(8,128)(2,1)} %shard_map.93.refs_6_), calls=%async_computation.3 | async-start | bytes 4194304 | tf_op jit(solution)/shard_map/all_to_all | solution.py:229
  127.2 4.8 %collective-permute-start.5 = (bf16[4,1024,128]{2,1,0:T(8,128)(2,1)}, bf16[4,1024,128]{2,1,0:T(8,128)(2,1)S(1)}, u32[]{:S(2)}, u32[]{:S(2)}) collective-permute-start(bf16[4,1024,128]{2,1,0:T(8,128)(2,1)} %project_out.2), channel_id=1, source_target_pairs={{0,1},{1,0},{2,3},{3,2},{4,5},{5,4},{6,7},{7,6},{8,9},{9,8},{10,11... | collective-permute-start | bytes 3145736 | tf_op jit(solution)/shard_map/ppermute | solution.py:242
  132.0 1.1 copy-start.1
  144.9 5.8 %copy-start = (bf16[4,256,1024]{2,1,0:T(8,128)(2,1)}, bf16[4,256,1024]{2,1,0:T(8,128)(2,1)S(1)}, u32[]{:S(2)}) copy-start(bf16[4,256,1024]{2,1,0:T(8,128)(2,1)S(1)} %all-to-all-done.3.d_parts) | copy-start | bytes 6291460
  144.9 23.7 %all-to-all-start.4 = ((bf16[16,256,128]{2,1,0:T(8,128)(2,1)}), bf16[16,256,128]{2,1,0:T(8,128)(2,1)S(1)}, u32[]{:S(2)}, u32[]{:S(2)}) async-start(bf16[16,256,128]{2,1,0:T(8,128)(2,1)} %bitcast.36), calls=%async_computation.4 | async-start | bytes 2097152 | tf_op jit(solution)/shard_map/all_to_all | solution.py:229
  157.9 16.5 %copy-start.3 = (f32[512,128]{1,0:T(8,128)S(1)}, f32[512,128]{1,0:T(8,128)}, u32[]{:S(2)}) copy-start(f32[512,128]{1,0:T(8,128)} %get-tuple-element.17) | copy-start | bytes 786436
  157.9 11.7 %collective-permute-start.7 = (bf16[512,128]{1,0:T(8,128)(2,1)}, bf16[512,128]{1,0:T(8,128)(2,1)S(1)}, u32[]{:S(2)}, u32[]{:S(2)}) collective-permute-start(bf16[512,128]{1,0:T(8,128)(2,1)} %get-tuple-element.19), channel_id=1, source_target_pairs={{8,0},{16,8},{24,16},{32,24},{40,32},{48,40},{56,48},{64,56},{72,6... | collective-permute-start | bytes 393224 | tf_op jit(solution)/shard_map/ppermute | solution.py:238
  165.8 8.6 %collective-permute-start.6 = (bf16[512,128]{1,0:T(8,128)(2,1)}, bf16[512,128]{1,0:T(8,128)(2,1)S(1)}, u32[]{:S(2)}, u32[]{:S(2)}) collective-permute-start(bf16[512,128]{1,0:T(8,128)(2,1)} %get-tuple-element.18), channel_id=1, source_target_pairs={{16,0},{24,8},{32,16},{40,24},{48,32},{56,40},{64,48},{72,56},{80,... | collective-permute-start | bytes 393224 | tf_op jit(solution)/shard_map/ppermute | solution.py:238
Sparse Core Ops, SparseCore 0:
  49.4 58.4 all-gather.1
